TPU v7x, 32 devices: a whole 2x2x4 slice. The times are simulated.
32 devices in a mesh: rows: 8 (over z, x), cols: 4 (over y, core).
Axes of the slice: x: 2, y: 2, z: 4, core: 2. Of those that a mesh axis runs over, the one named last changes fastest.
Arguments:
- vectors: bfloat16 [1024, 32768], P(None, 'rows'), may hold values from -0.4 to 0.4
- integrals: bfloat16 [2, 256, 32768], P(None, 'cols', 'rows'), may hold values from -8 to 72
- pivots: int32 [2, 256], replicated, may hold values from 0 to 32767, as said below
Outputs:
- new_vectors: float32 [2, 256, 32768], P(None, 'cols', 'rows')
Inputs may be any that keep to these rules, and one draw needn't show every extreme that they name: The 2 x 256 entries are distinct shell-pair rows. In each panel the rows of one index of rows (an aligned block of 4096) hold at most 64 pivots, and some block holds exactly 64.
All inputs are finite; a program needn't handle non-finite values.
Results may differ from a plain program's by a relative error of at most 0.00036.
Values may be sent and summed in bfloat16 or wider, within the bound.
No kernel may reach another device: no remote copies, remote signals or barrier semaphores. Data moves between devices by JAX's collectives and lax.ppermute only.
A program may use at most 64 MiB of HBM per device.

v0:
```python
import functools

import jax
import jax.numpy as jnp
from jax import lax
from jax.experimental import pallas as pl
from jax.experimental.pallas import tpu as pltpu
from jax.sharding import PartitionSpec as P

LANES = 128
LEAF = 32
SUB = 16
CHUNK = 512
SELECT = 1024
MICRO = 1 << 29
MIB = 1 << 20
ALMOST_ALL = 63 * MIB


def masks_of(size):
    return [1 << bit for bit in reversed(range(size.bit_length() - 1))]


def dot(left, right, left_dim=1, right_dim=0):
    return lax.dot_general(
        left, right, (((left_dim,), (right_dim,)), ((), ())), preferred_element_type=jnp.float32
    )


def split(x):
    high = x.astype(jnp.bfloat16)
    return high, (x - high.astype(jnp.float32)).astype(jnp.bfloat16)


def product_narrow(left, right, right_dim=0):
    rows = left.shape[0]
    both = dot(jnp.concatenate(split(left), 0), right, 1, right_dim)
    return both[:rows] + both[rows:]


def product_wide(left, right):
    left_high, left_low = split(left)
    right_high, right_low = split(right)
    return dot(
        jnp.concatenate([left_high, left_low, left_high], 1),
        jnp.concatenate([right_high, right_high, right_low], 0),
    )


def iota(shape, dim):
    return lax.broadcasted_iota(jnp.int32, shape, dim)


def as_column(row):
    size = row.shape[1]
    square = (size, size)
    return jnp.sum(
        jnp.where(iota(square, 0) == iota(square, 1), jnp.broadcast_to(row, square), 0.0),
        axis=1,
        keepdims=True,
    )


def pack(x):
    half = x.shape[0] // 2
    return jnp.concatenate([x[:half], x[half:]], 1)


def select_kernel(slot_count, pivots_ref, vectors_ref, integrals_ref, *refs):
    panels, block_cols, _ = integrals_ref.shape
    found_ref, out_refs = refs[0], refs[1 : 1 + panels]
    vec, ints, sems = refs[1 + panels :]
    part, row_count = vec.shape
    width = pivots_ref.shape[1]
    lanes = panels * slot_count
    first = pl.multiple_of(lax.axis_index("cols") * part, part)
    step = min(SELECT, row_count)
    count = row_count // step
    copies = []
    for n in range(count):
        at = pl.ds(n * step, step)
        copies.append(
            pltpu.make_async_copy(
                vectors_ref.at[pl.ds(first, part), at], vec.at[:, at], sems.at[n]
            )
        )
    whole = pltpu.make_async_copy(integrals_ref, ints, sems.at[count])
    for copy in copies[:1] + [whole] + copies[1:]:
        copy.start()
    start = (lax.axis_index("rows") * row_count).astype(jnp.float32)
    square = (width, width)
    target = jnp.zeros((1, lanes), jnp.float32)
    for panel in range(panels):
        local = pivots_ref[panel : panel + 1, :].astype(jnp.float32) - start
        mine = ((local >= 0.0) & (local < row_count)).astype(jnp.float32)
        earlier = iota(square, 1) < iota(square, 0)
        rank = jnp.sum(
            jnp.where(earlier, jnp.broadcast_to(mine, square), 0.0), axis=1, keepdims=True
        )
        held = as_column(jnp.where(mine > 0.0, local + 1.0, 0.0))
        slot = iota((width, lanes), 1).astype(jnp.float32) - panel * slot_count
        target = target + jnp.sum(jnp.where(rank == slot, held, 0.0), axis=0, keepdims=True)
    target = target.astype(jnp.int32) - 1
    whole.wait()
    outs = [
        pltpu.make_async_copy(ints.at[panel], out_refs[panel], sems.at[count + 1 + panel])
        for panel in range(panels)
    ]
    for copy in outs:
        copy.start()
    found = jnp.zeros((part + panels * block_cols, lanes), jnp.float32)
    for n, copy in enumerate(copies):
        copy.wait()
        at = slice(n * step, (n + 1) * step)
        pick = jnp.where(iota((step, lanes), 0) + n * step == target, 1.0, 0.0).astype(jnp.bfloat16)
        left = jnp.concatenate([vec[:, at]] + [ints[panel, :, at] for panel in range(panels)], 0)
        found = found + dot(left, pick)
    common = part + block_cols
    found_ref[:common, :] = found[:common].astype(jnp.bfloat16)
    found_ref[common:, :] = pack(found[common:, slot_count:]).astype(jnp.bfloat16)
    for copy in outs:
        copy.wait()


def select(pivots, vectors, integrals, slot_count, part):
    panels, block_cols, row_count = integrals.shape
    rows = part + block_cols + block_cols // 2
    outs = [jax.ShapeDtypeStruct((rows, panels * slot_count), jnp.bfloat16)]
    outs += [jax.ShapeDtypeStruct((block_cols, row_count), jnp.bfloat16)] * panels
    results = pl.pallas_call(
        functools.partial(select_kernel, slot_count),
        out_shape=outs,
        in_specs=[
            pl.BlockSpec(memory_space=pltpu.VMEM),
            pl.BlockSpec(memory_space=pltpu.HBM),
            pl.BlockSpec(memory_space=pltpu.HBM),
        ],
        out_specs=[pl.BlockSpec(memory_space=pltpu.VMEM)]
        + [pl.BlockSpec(memory_space=pltpu.HBM)] * panels,
        scratch_shapes=[
            pltpu.VMEM((part, row_count), jnp.bfloat16),
            pltpu.VMEM(integrals.shape, jnp.bfloat16),
            pltpu.SemaphoreType.DMA((row_count // min(SELECT, row_count) + 1 + panels,)),
        ],
        compiler_params=pltpu.CompilerParams(vmem_limit_bytes=ALMOST_ALL),
        cost_estimate=pl.CostEstimate(flops=MICRO * 2, bytes_accessed=3 * MIB, transcendentals=0),
        name="select",
    )(pivots, vectors, integrals)
    return results[0], results[1:]


def compact_kernel(weights, slot_count, row_count, pivots_ref, *refs):
    pieces, outs = refs[:-2], refs[-2:]
    panels, width = pivots_ref.shape
    depth, rows, lanes = pieces[0].shape
    common = outs[0].shape[0]
    shift = row_count.bit_length() - 1
    me = lax.axis_index("rows")
    square = (width, width)
    places = []
    for panel in range(panels):
        owner = lax.shift_right_logical(
            pivots_ref[panel : panel + 1, :], jnp.full((1, width), shift, jnp.int32)
        )
        floats = owner.astype(jnp.float32)
        same = jnp.broadcast_to(floats, square) == as_column(floats)
        earlier = iota(square, 0) < iota(square, 1)
        rank = jnp.sum(
            jnp.where(same & earlier, 1.0, 0.0), axis=0, keepdims=True
        ).astype(jnp.int32)
        apart = owner ^ me
        block = jnp.zeros_like(owner)
        for mask, weight in weights:
            block = block + jnp.where((apart & mask) != 0, weight, 0)
        places.append(block * lanes + rank)
    both = jnp.concatenate([places[0], places[1] + slot_count], 1)
    halves = jnp.concatenate([places[1], places[1] + slot_count], 1)
    main = jnp.zeros((common, 2 * width), jnp.float32)
    rest = jnp.zeros((rows - common, 2 * width), jnp.float32)
    for i in range(len(pieces) * depth):
        lane = iota((lanes, 2 * width), 0) + i * lanes
        x = pieces[i // depth][i % depth]
        main = main + dot(x[:common], jnp.where(lane == both, 1.0, 0.0).astype(jnp.bfloat16))
        rest = rest + dot(x[common:], jnp.where(lane == halves, 1.0, 0.0).astype(jnp.bfloat16))
    outs[0][...] = main[:, :width].astype(jnp.bfloat16)
    outs[1][:common, :] = main[:, width:].astype(jnp.bfloat16)
    outs[1][common : common + rows - common, :] = rest[:, :width].astype(jnp.bfloat16)
    outs[1][rows:, :] = rest[:, width:].astype(jnp.bfloat16)


def compact(pivots, pieces, weights, slot_count, row_count, part):
    _, rows, _ = pieces[0].shape
    width = pivots.shape[1]
    block_cols = (rows - part) * 2 // 3
    return pl.pallas_call(
        functools.partial(compact_kernel, weights, slot_count, row_count),
        out_shape=[
            jax.ShapeDtypeStruct((part + block_cols, width), jnp.bfloat16),
            jax.ShapeDtypeStruct((part + 2 * block_cols, width), jnp.bfloat16),
        ],
        in_specs=[pl.BlockSpec(memory_space=pltpu.VMEM)] * (1 + len(pieces)),
        out_specs=[pl.BlockSpec(memory_space=pltpu.VMEM)] * 2,
        compiler_params=pltpu.CompilerParams(vmem_limit_bytes=16 * MIB),
        cost_estimate=pl.CostEstimate(flops=MICRO, bytes_accessed=MIB, transcendentals=0),
        name="compact",
    )(pivots, *pieces)


def eliminate(block, columns, offset):
    vregs = LEAF // 8
    tiles = {g: [x[8 * v : 8 * v + 8] for v in range(vregs)] for g, x in block.items()}
    sublane = iota((8, LANES), 0)
    pivots = [jnp.zeros((8, LANES), jnp.float32) for _ in range(vregs)]
    for sub in range(0, LEAF, SUB):
        first = sub // 8
        diagonal = tiles[columns][first:]
        cols = [
            [
                jnp.broadcast_to(x[:, offset + sub + k : offset + sub + k + 1], (8, LANES))
                for x in diagonal
            ]
            for k in range(SUB)
        ]
        for j in range(SUB):
            jv, jr = j // 8, j % 8
            live = range(jv, len(diagonal))
            pivot = jnp.broadcast_to(cols[j][jv][jr : jr + 1, :], (8, LANES))
            inverse = 1.0 / pivot
            factor = {v: cols[j][v] * inverse for v in live}
            factor[jv] = jnp.where(sublane > jr, factor[jv], 0.0)
            pivots[first + jv] = jnp.where(sublane == jr, pivot, pivots[first + jv])
            for k in range(j + 1, SUB):
                entry = jnp.broadcast_to(cols[k][jv][jr : jr + 1, :], (8, LANES))
                for v in live:
                    cols[k][v] = cols[k][v] - factor[v] * entry
            for rows in tiles.values():
                entry = jnp.broadcast_to(rows[first + jv][jr : jr + 1, :], (8, LANES))
                for v in live:
                    rows[first + v] = rows[first + v] - factor[v] * entry
    scale = [lax.rsqrt(pivot) for pivot in pivots]
    return {
        g: jnp.concatenate([x * y for x, y in zip(rows, scale)], 0) for g, rows in tiles.items()
    }


def start_factor(matrix, work):
    width = matrix.shape[0]
    square = (width, width)
    work[:, :width] = 0.5 * (matrix + matrix.T)
    work[:, width:] = jnp.where(iota(square, 0) == iota(square, 1), 1.0, 0.0)


def lanes_of(g):
    return slice(g * LANES, (g + 1) * LANES)


def run_leaves(work, begin, end):
    width = work.shape[0]
    half = width // LANES
    block = None
    for start in range(begin, end, LEAF):
        following = start + LEAF
        rights = [half + g for g in range((following - 1) // LANES + 1)]
        groups = list(range(start // LANES, half)) + rights
        if block is None:
            block = {g: work[start:following, lanes_of(g)] for g in groups}
        upper = eliminate(block, start // LANES, start % LANES)
        for g in rights:
            work[start:following, lanes_of(g)] = upper[g]
        if following == width:
            break
        lefts = list(range(following // LANES, half))
        used = lefts + rights
        base = lefts[0] * LANES
        high, low = split(jnp.concatenate([upper[g] for g in used], 1))
        right = jnp.concatenate([high, high, low], 0)

        def product(first, last):
            a = high[:, first - base : last - base]
            b = low[:, first - base : last - base]
            return dot(jnp.concatenate([a, b, a], 0), right, 0, 0)

        stop = following + LEAF
        change = product(following, stop)
        block = {}
        for g in lefts + [half + g for g in range((stop - 1) // LANES + 1)]:
            block[g] = work[following:stop, lanes_of(g)]
            if g in used:
                block[g] = block[g] - change[:, lanes_of(used.index(g))]
        if following == end:
            for g, x in block.items():
                work[following:stop, lanes_of(g)] = x
        if stop < width:
            change = product(stop, width)
            for i, g in enumerate(used):
                work[stop:, lanes_of(g)] = work[stop:, lanes_of(g)] - change[:, lanes_of(i)]


def first_kernel(apart, part, *refs):
    count = len(apart)
    picked = refs[:count]
    work, rows_of, ints = refs[count:]
    me = lax.axis_index("cols")
    block_cols = picked[0].shape[0] - part
    for ref, bits in zip(picked, apart):
        at = pl.multiple_of((me ^ bits) * block_cols, block_cols)
        rows_of[pl.ds(pl.multiple_of((me ^ bits) * part, part), part), :] = ref[:part, :]
        ints[pl.ds(at, block_cols), :] = ref[part:, :].astype(jnp.float32)
    at_pivots = rows_of[...]
    start_factor(ints[...] - dot(at_pivots, at_pivots, 0, 0), work)
    run_leaves(work, 0, work.shape[0] // 2)


def first_half(picked, apart, part):
    count = len(apart)
    _, width = picked[0].shape
    return pl.pallas_call(
        functools.partial(first_kernel, apart, part),
        out_shape=jax.ShapeDtypeStruct((width, 2 * width), jnp.float32),
        in_specs=[pl.BlockSpec(memory_space=pltpu.VMEM)] * count,
        out_specs=pl.BlockSpec(memory_space=pltpu.VMEM),
        scratch_shapes=[
            pltpu.VMEM((count * part, width), jnp.bfloat16),
            pltpu.VMEM((width, width), jnp.float32),
        ],
        compiler_params=pltpu.CompilerParams(vmem_limit_bytes=16 * MIB),
        cost_estimate=pl.CostEstimate(flops=4 * MICRO, bytes_accessed=MIB, transcendentals=0),
        name="first_half",
    )(*picked)


def second_kernel(before_ref, work):
    work[...] = before_ref[...]
    run_leaves(work, work.shape[0] // 2, work.shape[0])


def second_half(work):
    return pl.pallas_call(
        second_kernel,
        out_shape=jax.ShapeDtypeStruct(work.shape, work.dtype),
        in_specs=[pl.BlockSpec(memory_space=pltpu.VMEM)],
        out_specs=pl.BlockSpec(memory_space=pltpu.VMEM),
        compiler_params=pltpu.CompilerParams(vmem_limit_bytes=16 * MIB),
        cost_estimate=pl.CostEstimate(flops=4 * MICRO, bytes_accessed=MIB, transcendentals=0),
        name="second_half",
    )(work)


def third_kernel(apart, part, *refs):
    count = len(apart)
    work0, picked0, picked1 = refs[0], refs[1 : 1 + count], refs[1 + count : 1 + 2 * count]
    work1, rows_of, ahead_ref, ints0, ints1 = refs[1 + 2 * count :]
    me = lax.axis_index("cols")
    width = work0.shape[0]
    block_cols = picked0[0].shape[0] - part
    for i, bits in enumerate(apart):
        at = pl.ds(pl.multiple_of((me ^ bits) * part, part), part)
        rows_of[at, :width] = picked0[i][:part, :]
        rows_of[at, width:] = picked1[i][:part, :]
        at = pl.ds(pl.multiple_of((me ^ bits) * block_cols, block_cols), block_cols)
        ints0[at, :] = picked1[i][part : part + block_cols, :].astype(jnp.float32)
        ints1[at, :] = picked1[i][part + block_cols :, :].astype(jnp.float32)
    gram = dot(rows_of[...], rows_of[:, width:], 0, 0)
    ahead = product_wide(work0[:, width:], ints0[...] - gram[:width]).astype(jnp.bfloat16)
    ahead_ref[...] = ahead
    start_factor(ints1[...] - gram[width:] - dot(ahead, ahead, 0, 0), work1)
    run_leaves(work1, 0, width // 2)


def third_half(work0, picked0, picked1, apart, part):
    count = len(apart)
    width = work0.shape[0]
    return pl.pallas_call(
        functools.partial(third_kernel, apart, part),
        out_shape=[
            jax.ShapeDtypeStruct(work0.shape, jnp.float32),
            jax.ShapeDtypeStruct((count * part, 2 * width), jnp.bfloat16),
            jax.ShapeDtypeStruct((width, width), jnp.bfloat16),
        ],
        in_specs=[pl.BlockSpec(memory_space=pltpu.VMEM)] * (1 + 2 * count),
        out_specs=[pl.BlockSpec(memory_space=pltpu.VMEM)] * 3,
        scratch_shapes=[pltpu.VMEM((width, width), jnp.float32)] * 2,
        compiler_params=pltpu.CompilerParams(vmem_limit_bytes=16 * MIB),
        cost_estimate=pl.CostEstimate(flops=5 * MICRO, bytes_accessed=MIB, transcendentals=0),
        name="third_half",
    )(work0, *picked0, *picked1)


def fourth_kernel(block_cols, work0, before_ref, rows_of, ahead, left, work1):
    width = work0.shape[0]
    both = 2 * width
    work1[...] = before_ref[...]
    run_leaves(work1, width // 2, width)
    me = lax.axis_index("cols")
    mine = pl.ds(pl.multiple_of(me * block_cols, block_cols), block_cols)
    inverse0 = work0[mine, width:]
    inverse1 = work1[mine, width:]
    through = product_wide(product_narrow(inverse1, ahead[...], 1), work0[:, width:])
    small = jnp.concatenate(
        [
            jnp.concatenate([inverse0, jnp.zeros_like(inverse0)], 1),
            jnp.concatenate([-through, inverse1], 1),
        ],
        0,
    )
    left[:, :both] = jnp.concatenate(split(small), 0)
    left[:, both:] = jnp.concatenate(split(-product_narrow(small, rows_of[...], 1)), 0)


def fourth_half(work0, work1, rows_of, ahead, block_cols):
    width = work0.shape[0]
    return pl.pallas_call(
        functools.partial(fourth_kernel, block_cols),
        out_shape=jax.ShapeDtypeStruct(
            (4 * block_cols, 2 * width + rows_of.shape[0]), jnp.bfloat16
        ),
        in_specs=[pl.BlockSpec(memory_space=pltpu.VMEM)] * 4,
        out_specs=pl.BlockSpec(memory_space=pltpu.VMEM),
        scratch_shapes=[pltpu.VMEM(work0.shape, jnp.float32)],
        compiler_params=pltpu.CompilerParams(vmem_limit_bytes=16 * MIB),
        cost_estimate=pl.CostEstimate(flops=5 * MICRO, bytes_accessed=MIB, transcendentals=0),
        name="fourth_half",
    )(work0, work1, rows_of, ahead)


def finish_kernel(apart, *refs):
    count = len(apart)
    left, vectors_ref = refs[0], refs[1]
    blocks = refs[2 : 2 + 2 * count]
    out_ref, right, result, sems, out_sems = refs[2 + 2 * count :]
    me = lax.axis_index("cols")
    pairs = vectors_ref.shape[1]
    block_cols = blocks[0].shape[0]
    both = right.shape[0]
    copies = []
    for n in range(pairs // CHUNK):
        for i, ref in enumerate(blocks):
            place = i // count * (both // 2) + (me ^ apart[i % count]) * block_cols
            rows = pl.ds(pl.multiple_of(place, block_cols), block_cols)
            at = pl.ds(n * CHUNK, CHUNK)
            copies.append(
                pltpu.make_async_copy(ref.at[:, at], right.at[rows, at], sems.at[n, i])
            )
            copies[-1].start()
    outs = []
    for n in range(pairs // CHUNK):
        at = pl.ds(n * CHUNK, CHUNK)
        for copy in copies[n * len(blocks) : (n + 1) * len(blocks)]:
            copy.wait()
        halves = dot(left[:, both:], vectors_ref[:, at]) + dot(left[:, :both], right[:, at])
        value = halves[: 2 * block_cols] + halves[2 * block_cols :]
        result[0, :, at] = value[:block_cols]
        result[1, :, at] = value[block_cols:]
        outs.append(
            pltpu.make_async_copy(result.at[:, :, at], out_ref.at[:, :, at], out_sems.at[n])
        )
        outs[-1].start()
    for copy in outs:
        copy.wait()


def finish(left, vectors, blocks, apart):
    block_cols, pairs = blocks[0].shape
    both = left.shape[1] - vectors.shape[0]
    return pl.pallas_call(
        functools.partial(finish_kernel, apart),
        out_shape=jax.ShapeDtypeStruct((2, block_cols, pairs), jnp.float32),
        in_specs=[pl.BlockSpec(memory_space=pltpu.VMEM)] * 2
        + [pl.BlockSpec(memory_space=pl.ANY)] * len(blocks),
        out_specs=pl.BlockSpec(memory_space=pl.ANY),
        scratch_shapes=[
            pltpu.VMEM((both, pairs), jnp.bfloat16),
            pltpu.VMEM((2, block_cols, pairs), jnp.float32),
            pltpu.SemaphoreType.DMA((pairs // CHUNK, len(blocks))),
            pltpu.SemaphoreType.DMA((pairs // CHUNK,)),
        ],
        compiler_params=pltpu.CompilerParams(vmem_limit_bytes=24 * MIB),
        cost_estimate=pl.CostEstimate(
            flops=6 * MICRO, bytes_accessed=16 * MIB, transcendentals=0
        ),
        name="finish",
    )(left, vectors, *blocks)


def per_device(vectors, integrals, pivots):
    prior, row_count = vectors.shape
    _, width = pivots.shape
    owners, col_count = lax.axis_size("rows"), lax.axis_size("cols")
    block_cols = integrals.shape[1]
    slot_count = 2 * width // owners
    part = prior // col_count

    def swap(x, axis, mask):
        size = lax.axis_size(axis)
        return lax.ppermute(x, axis, [(i, i ^ mask) for i in range(size)])

    def near(pieces):
        return [swap(piece, "cols", near_mask) for piece in pieces]

    far_mask, near_mask = masks_of(col_count)
    apart = [0, far_mask, near_mask, far_mask ^ near_mask]

    found, ints = select(pivots, vectors, integrals, slot_count, part)
    masks = masks_of(owners)
    held = found[None]
    depth, weights = 1, []
    for mask in masks[:-3]:
        held = jnp.concatenate([held, swap(held, "rows", mask)], 0)
        weights.append((mask, depth))
        depth = 2 * depth
    weights += [(mask, depth << i) for i, mask in enumerate(masks[-3:])]
    passed = swap(held, "rows", masks[-3])
    pieces = [held, passed]
    for mask in (masks[-2], masks[-1], masks[-2] ^ masks[-1]):
        pieces.append(swap(held, "rows", mask))
        pieces.append(swap(passed, "rows", mask))
    own0, own1 = compact(pivots, pieces, weights, slot_count, row_count, part)

    far0 = swap(ints[0], "cols", far_mask)
    other0 = swap(own0, "cols", far_mask)
    other1 = swap(own1, "cols", far_mask)
    pair1 = [own1, other1]
    picked0 = [own0, other0] + near([own0]) + near([other0])
    picked0, last = lax.optimization_barrier((picked0, ints[1]))
    far1 = swap(last, "cols", far_mask)
    work0 = first_half(picked0, apart, part)
    work0, pair1, ints0 = lax.optimization_barrier((work0, pair1, [ints[0], far0]))
    picked1 = pair1 + near(pair1)
    blocks = ints0 + near(ints0)
    work0 = second_half(work0)
    work1, rows_of, ahead = third_half(work0, picked0, picked1, apart, part)
    work1, ints1 = lax.optimization_barrier((work1, [last, far1]))
    blocks += ints1 + near(ints1)
    left = fourth_half(work0, work1, rows_of, ahead, block_cols)
    return finish(left, vectors, blocks, apart)


def solution(mesh):
    placed = (P(None, "rows"), P(None, "cols", "rows"), P())

    return jax.shard_map(
        per_device, mesh=mesh, in_specs=placed, out_specs=P(None, "cols", "rows"), check_vma=False
    )
```

profile of v0, /device:TPU:0, one launch (start us, length us, event | category | flops | bytes accessed | tf_op | source)
XLA Modules:
  0.0 66.7 jit_solution(11988081166137674379)
XLA Ops:
  0.0 5.0 %select.1 = (bf16[352,128]{1,0:T(8,128)(2,1)}, bf16[64,4096]{1,0:T(8,128)(2,1)}, bf16[64,4096]{1,0:T(8,128)(2,1)}) custom-call(s32[2,256]{1,0:T(2,128)} %pivots_ref.3, bf16[1024,4096]{1,0:T(8,128)(2,1)} %refs_1_.1, bf16[2,64,4096]{2,1,0:T(8,128)(2,1)} %integrals_ref.1), custom_call_target="tpu_custom_call" | custom-call | flops 1073741824 | bytes 3145728 | tf_op jit(solution)/shard_map/select/pallas_call | solution.py:130
  5.0 4.1 %collective-permute-start = (bf16[1,352,128]{2,1,0:T(8,128)(2,1)}, bf16[1,352,128]{2,1,0:T(8,128)(2,1)S(1)}, u32[]{:S(2)}, u32[]{:S(2)}) collective-permute-start(bf16[1,352,128]{2,1,0:T(8,128)(2,1)} %bitcast.3), channel_id=1, source_target_pairs={{0,16},{4,20},{8,24},{12,28},{16,0},{20,4},{24,8},{28,12},{1,17},{... | collective-permute-start | bytes 270344 | tf_op jit(solution)/shard_map/ppermute | solution.py:495
  9.1 2.5 %collective-permute-start.5 = (bf16[1,352,128]{2,1,0:T(8,128)(2,1)}, bf16[1,352,128]{2,1,0:T(8,128)(2,1)S(1)}, u32[]{:S(2)}, u32[]{:S(2)}) collective-permute-start(bf16[1,352,128]{2,1,0:T(8,128)(2,1)} %bitcast.4), channel_id=1, source_target_pairs={{0,12},{4,8},{8,4},{12,0},{16,28},{20,24},{24,20},{28,16},{1,13},{... | collective-permute-start | bytes 270344 | tf_op jit(solution)/shard_map/ppermute | solution.py:495
  11.6 0.5 collective-permute-start.3
  12.6 1.0 %collective-permute-done.refs_1_ = bf16[1,352,128]{2,1,0:T(8,128)(2,1)S(1)} collective-permute-done((bf16[1,352,128]{2,1,0:T(8,128)(2,1)}, bf16[1,352,128]{2,1,0:T(8,128)(2,1)S(1)}, u32[]{:S(2)}, u32[]{:S(2)}) %collective-permute-start) | collective-permute-done | bytes 90144 | tf_op jit(solution)/shard_map/ppermute | solution.py:495
  13.6 2.0 %collective-permute-start.6 = (bf16[1,352,128]{2,1,0:T(8,128)(2,1)S(1)}, bf16[1,352,128]{2,1,0:T(8,128)(2,1)S(1)}, u32[]{:S(2)}, u32[]{:S(2)}) collective-permute-start(bf16[1,352,128]{2,1,0:T(8,128)(2,1)S(1)} %collective-permute-done.refs_1_), channel_id=1, source_target_pairs={{0,12},{4,8},{8,4},{12,0},{16,28},{20,24},{24,20},{28,16},{1,13},{... | collective-permute-start | bytes 270344 | tf_op jit(solution)/shard_map/ppermute | solution.py:495
  15.7 0.6 collective-permute-start.4
  16.2 1.3 %collective-permute-start.2 = (bf16[1,352,128]{2,1,0:T(8,128)(2,1)S(1)}, bf16[1,352,128]{2,1,0:T(8,128)(2,1)S(1)}, u32[]{:S(2)}, u32[]{:S(2)}) collective-permute-start(bf16[1,352,128]{2,1,0:T(8,128)(2,1)S(1)} %collective-permute-done.refs_1_), channel_id=1, source_target_pairs={{0,8},{4,12},{8,0},{12,4},{16,24},{20,28},{24,16},{28,20},{1,9},{5... | collective-permute-start | bytes 270344 | tf_op jit(solution)/shard_map/ppermute | solution.py:495
  17.9 1.6 %collective-permute-done.6.refs_7_ = bf16[1,352,128]{2,1,0:T(8,128)(2,1)S(1)} collective-permute-done((bf16[1,352,128]{2,1,0:T(8,128)(2,1)S(1)}, bf16[1,352,128]{2,1,0:T(8,128)(2,1)S(1)}, u32[]{:S(2)}, u32[]{:S(2)}) %collective-permute-start.6) | collective-permute-done | bytes 90144 | tf_op jit(solution)/shard_map/ppermute | solution.py:495
  19.4 1.2 %collective-permute-done.4.refs_5_ = bf16[1,352,128]{2,1,0:T(8,128)(2,1)S(1)} collective-permute-done((bf16[1,352,128]{2,1,0:T(8,128)(2,1)S(1)}, bf16[1,352,128]{2,1,0:T(8,128)(2,1)S(1)}, u32[]{:S(2)}, u32[]{:S(2)}) %collective-permute-start.4) | collective-permute-done | bytes 90144 | tf_op jit(solution)/shard_map/ppermute | solution.py:495
  21.1 0.9 %copy-done.3 = bf16[352,128]{1,0:T(8,128)(2,1)S(1)} copy-done((bf16[352,128]{1,0:T(8,128)(2,1)S(1)}, bf16[352,128]{1,0:T(8,128)(2,1)}, u32[]{:S(2)}) %copy-start.3) | copy-done | bytes 90136
  22.0 1.1 %compact.1 = (bf16[320,256]{1,0:T(8,128)(2,1)S(1)}, bf16[384,256]{1,0:T(8,128)(2,1)S(1)}) custom-call(s32[2,256]{1,0:T(2,128)S(1)} %copy-done.2, bf16[1,352,128]{2,1,0:T(8,128)(2,1)S(1)} %bitcast.7, bf16[1,352,128]{2,1,0:T(8,128)(2,1)S(1)} %collective-permute-done.refs_1_, bf16[1,352,128]{2,1,0:T(8,128)(2,1)S(1)} %collective-permute-done.1.refs_2_, ...), custom_call_target="tpu_custom_call" | custom-call | flops 536870912 | bytes 1048576 | tf_op jit(solution)/shard_map/compact/pallas_call | solution.py:195
  23.2 1.6 %collective-permute-start.7 = (bf16[320,256]{1,0:T(8,128)(2,1)S(1)}, bf16[320,256]{1,0:T(8,128)(2,1)S(1)}, u32[]{:S(2)}, u32[]{:S(2)}) collective-permute-start(bf16[320,256]{1,0:T(8,128)(2,1)S(1)} %get-tuple-element.29.refs_0_.refs_1_), channel_id=1, source_target_pairs={{0,2},{1,3},{2,0},{3,1},{4,6},{5,7},{6,4},{7,5},{8,10},{9,11},{10,... | collective-permute-start | bytes 491528 | tf_op jit(solution)/shard_map/ppermute | solution.py:495
  25.3 5.0 %collective-permute-done.7.refs_1_.refs_2_ = bf16[320,256]{1,0:T(8,128)(2,1)S(1)} collective-permute-done((bf16[320,256]{1,0:T(8,128)(2,1)S(1)}, bf16[320,256]{1,0:T(8,128)(2,1)S(1)}, u32[]{:S(2)}, u32[]{:S(2)}) %collective-permute-start.7) | collective-permute-done | bytes 163872 | tf_op jit(solution)/shard_map/ppermute | solution.py:495
  30.3 1.5 %collective-permute-start.10 = (bf16[384,256]{1,0:T(8,128)(2,1)S(1)}, bf16[384,256]{1,0:T(8,128)(2,1)S(1)}, u32[]{:S(2)}, u32[]{:S(2)}) collective-permute-start(bf16[384,256]{1,0:T(8,128)(2,1)S(1)} %get-tuple-element.36.refs_5_), channel_id=1, source_target_pairs={{0,2},{1,3},{2,0},{3,1},{4,6},{5,7},{6,4},{7,5},{8,10},{9,11},{10,... | collective-permute-start | bytes 589832 | tf_op jit(solution)/shard_map/ppermute | solution.py:495
  31.8 1.4 %collective-permute-start.14 = (bf16[64,4096]{1,0:T(8,128)(2,1)}, bf16[64,4096]{1,0:T(8,128)(2,1)S(1)}, u32[]{:S(2)}, u32[]{:S(2)}) collective-permute-start(bf16[64,4096]{1,0:T(8,128)(2,1)} %get-tuple-element.45.refs_6_), channel_id=1, source_target_pairs={{0,2},{1,3},{2,0},{3,1},{4,6},{5,7},{6,4},{7,5},{8,10},{9,11},{10,... | collective-permute-start | bytes 1572872 | tf_op jit(solution)/shard_map/ppermute | solution.py:495
  33.2 4.0 %first_half.1.before_ref = f32[256,512]{1,0:T(8,128)S(1)} custom-call(bf16[320,256]{1,0:T(8,128)(2,1)S(1)} %get-tuple-element.29.refs_0_.refs_1_, bf16[320,256]{1,0:T(8,128)(2,1)S(1)} %collective-permute-done.7.refs_1_.refs_2_, bf16[320,256]{1,0:T(8,128)(2,1)S(1)} %collective-permute-done.8.refs_2_.refs_3_, ...), custom_call_target="tpu_custom_call" | custom-call | flops 2147483648 | bytes 1048576 | tf_op jit(solution)/shard_map/first_half/pallas_call | solution.py:317
  37.2 8.6 %collective-permute-done.10.refs_6_ = bf16[384,256]{1,0:T(8,128)(2,1)S(1)} collective-permute-done((bf16[384,256]{1,0:T(8,128)(2,1)S(1)}, bf16[384,256]{1,0:T(8,128)(2,1)S(1)}, u32[]{:S(2)}, u32[]{:S(2)}) %collective-permute-start.10) | collective-permute-done | bytes 196640 | tf_op jit(solution)/shard_map/ppermute | solution.py:495
  45.8 0.5 collective-permute-start.13
  46.3 0.5 collective-permute-start.16
  46.8 3.2 %second_half.1.refs_0_.work0 = f32[256,512]{1,0:T(8,128)S(1)} custom-call(f32[256,512]{1,0:T(8,128)S(1)} %first_half.1.before_ref), custom_call_target="tpu_custom_call" | custom-call | flops 2147483648 | bytes 1048576 | tf_op jit(solution)/shard_map/second_half/pallas_call | solution.py:338
  50.0 4.7 %third_half.1 = (f32[256,512]{1,0:T(8,128)S(1)}, bf16[1024,512]{1,0:T(8,128)(2,1)S(1)}, bf16[256,256]{1,0:T(8,128)(2,1)S(1)}) custom-call(f32[256,512]{1,0:T(8,128)S(1)} %second_half.1.refs_0_.work0, bf16[320,256]{1,0:T(8,128)(2,1)S(1)} %get-tuple-element.29.refs_0_.refs_1_, bf16[320,256]{1,0:T(8,128)(2,1)S(1)} %collective-permute-done.7.refs_1_.refs_2_, ...), custom_call_target="tpu_custom_call" | custom-call | flops 2684354560 | bytes 1048576 | tf_op jit(solution)/shard_map/third_half/pallas_call | solution.py:373
  55.6 4.1 %fourth_half.1.refs_0_ = bf16[256,1536]{1,0:T(8,128)(2,1)S(1)} custom-call(f32[256,512]{1,0:T(8,128)S(1)} %second_half.1.refs_0_.work0, f32[256,512]{1,0:T(8,128)S(1)} %get-tuple-element.40.before_ref, bf16[1024,512]{1,0:T(8,128)(2,1)S(1)} %get-tuple-element.41.rows_of, bf16[256,256]{1,0:T(8,128)(2,1)S(1)} %get-tuple-element.42.ahead), custom_call_target="tpu_custom_call" | custom-call | flops 2684354560 | bytes 1048576 | tf_op jit(solution)/shard_map/fourth_half/pallas_call | solution.py:412
  59.8 6.8 %finish.1 = f32[2,64,4096]{2,1,0:T(8,128)} custom-call(bf16[256,1536]{1,0:T(8,128)(2,1)S(1)} %fourth_half.1.refs_0_, bf16[1024,4096]{1,0:T(8,128)(2,1)S(1)} %bitcast.2, bf16[64,4096]{1,0:T(8,128)(2,1)S(1)} %copy-done, bf16[64,4096]{1,0:T(8,128)(2,1)S(1)} %collective-permute-done.11.refs_3_, bf16[64,4096]{1,0:T(8,128)(2,1)S(1)} %collective-permute-done.15.refs_4_, ...), custom_call_target="tpu_custom_call" | custom-call | flops 3221225472 | bytes 16777216 | tf_op jit(solution)/shard_map/finish/pallas_call | solution.py:465
  (34 shorter events, 2.6 us)
Async XLA Ops:
  0.0 21.1 %copy-start.2 = (s32[2,256]{1,0:T(2,128)S(1)}, s32[2,256]{1,0:T(2,128)}, u32[]{:S(2)}) copy-start(s32[2,256]{1,0:T(2,128)} %pivots_ref.3) | copy-start | bytes 6148
  5.0 41.3 %copy-start = (bf16[64,4096]{1,0:T(8,128)(2,1)S(1)}, bf16[64,4096]{1,0:T(8,128)(2,1)}, u32[]{:S(2)}) copy-start(bf16[64,4096]{1,0:T(8,128)(2,1)} %get-tuple-element.43.refs_2_) | copy-start | bytes 1572868
  5.0 8.6 %collective-permute-start = (bf16[1,352,128]{2,1,0:T(8,128)(2,1)}, bf16[1,352,128]{2,1,0:T(8,128)(2,1)S(1)}, u32[]{:S(2)}, u32[]{:S(2)}) collective-permute-start(bf16[1,352,128]{2,1,0:T(8,128)(2,1)} %bitcast.3), channel_id=1, source_target_pairs={{0,16},{4,20},{8,24},{12,28},{16,0},{20,4},{24,8},{28,12},{1,17},{... | collective-permute-start | bytes 270344 | tf_op jit(solution)/shard_map/ppermute | solution.py:495
  9.1 7.1 %collective-permute-start.5 = (bf16[1,352,128]{2,1,0:T(8,128)(2,1)}, bf16[1,352,128]{2,1,0:T(8,128)(2,1)S(1)}, u32[]{:S(2)}, u32[]{:S(2)}) collective-permute-start(bf16[1,352,128]{2,1,0:T(8,128)(2,1)} %bitcast.4), channel_id=1, source_target_pairs={{0,12},{4,8},{8,4},{12,0},{16,28},{20,24},{24,20},{28,16},{1,13},{... | collective-permute-start | bytes 270344 | tf_op jit(solution)/shard_map/ppermute | solution.py:495
  11.6 6.0 %collective-permute-start.3 = (bf16[1,352,128]{2,1,0:T(8,128)(2,1)}, bf16[1,352,128]{2,1,0:T(8,128)(2,1)S(1)}, u32[]{:S(2)}, u32[]{:S(2)}) collective-permute-start(bf16[1,352,128]{2,1,0:T(8,128)(2,1)} %bitcast.5), channel_id=1, source_target_pairs={{0,4},{4,0},{8,12},{12,8},{16,20},{20,16},{24,28},{28,24},{1,5},{5... | collective-permute-start | bytes 270344 | tf_op jit(solution)/shard_map/ppermute | solution.py:495
  12.2 5.7 %collective-permute-start.1 = (bf16[1,352,128]{2,1,0:T(8,128)(2,1)}, bf16[1,352,128]{2,1,0:T(8,128)(2,1)S(1)}, u32[]{:S(2)}, u32[]{:S(2)}) collective-permute-start(bf16[1,352,128]{2,1,0:T(8,128)(2,1)} %bitcast.6), channel_id=1, source_target_pairs={{0,8},{4,12},{8,0},{12,4},{16,24},{20,28},{24,16},{28,20},{1,9},{5... | collective-permute-start | bytes 270344 | tf_op jit(solution)/shard_map/ppermute | solution.py:495
  13.6 5.8 %collective-permute-start.6 = (bf16[1,352,128]{2,1,0:T(8,128)(2,1)S(1)}, bf16[1,352,128]{2,1,0:T(8,128)(2,1)S(1)}, u32[]{:S(2)}, u32[]{:S(2)}) collective-permute-start(bf16[1,352,128]{2,1,0:T(8,128)(2,1)S(1)} %collective-permute-done.refs_1_), channel_id=1, source_target_pairs={{0,12},{4,8},{8,4},{12,0},{16,28},{20,24},{24,20},{28,16},{1,13},{... | collective-permute-start | bytes 270344 | tf_op jit(solution)/shard_map/ppermute | solution.py:495
  15.7 5.0 %collective-permute-start.4 = (bf16[1,352,128]{2,1,0:T(8,128)(2,1)S(1)}, bf16[1,352,128]{2,1,0:T(8,128)(2,1)S(1)}, u32[]{:S(2)}, u32[]{:S(2)}) collective-permute-start(bf16[1,352,128]{2,1,0:T(8,128)(2,1)S(1)} %collective-permute-done.refs_1_), channel_id=1, source_target_pairs={{0,4},{4,0},{8,12},{12,8},{16,20},{20,16},{24,28},{28,24},{1,5},{5... | collective-permute-start | bytes 270344 | tf_op jit(solution)/shard_map/ppermute | solution.py:495
  16.2 4.9 %collective-permute-start.2 = (bf16[1,352,128]{2,1,0:T(8,128)(2,1)S(1)}, bf16[1,352,128]{2,1,0:T(8,128)(2,1)S(1)}, u32[]{:S(2)}, u32[]{:S(2)}) collective-permute-start(bf16[1,352,128]{2,1,0:T(8,128)(2,1)S(1)} %collective-permute-done.refs_1_), channel_id=1, source_target_pairs={{0,8},{4,12},{8,0},{12,4},{16,24},{20,28},{24,16},{28,20},{1,9},{5... | collective-permute-start | bytes 270344 | tf_op jit(solution)/shard_map/ppermute | solution.py:495
  23.2 7.1 %collective-permute-start.7 = (bf16[320,256]{1,0:T(8,128)(2,1)S(1)}, bf16[320,256]{1,0:T(8,128)(2,1)S(1)}, u32[]{:S(2)}, u32[]{:S(2)}) collective-permute-start(bf16[320,256]{1,0:T(8,128)(2,1)S(1)} %get-tuple-element.29.refs_0_.refs_1_), channel_id=1, source_target_pairs={{0,2},{1,3},{2,0},{3,1},{4,6},{5,7},{6,4},{7,5},{8,10},{9,11},{10,... | collective-permute-start | bytes 491528 | tf_op jit(solution)/shard_map/ppermute | solution.py:495
  24.8 21.0 %collective-permute-start.11 = (bf16[64,4096]{1,0:T(8,128)(2,1)}, bf16[64,4096]{1,0:T(8,128)(2,1)S(1)}, u32[]{:S(2)}, u32[]{:S(2)}) collective-permute-start(bf16[64,4096]{1,0:T(8,128)(2,1)} %get-tuple-element.43.refs_2_), channel_id=1, source_target_pairs={{0,2},{1,3},{2,0},{3,1},{4,6},{5,7},{6,4},{7,5},{8,10},{9,11},{10,... | collective-permute-start | bytes 1572872 | tf_op jit(solution)/shard_map/ppermute | solution.py:495
  25.3 6.6 %collective-permute-start.8 = (bf16[320,256]{1,0:T(8,128)(2,1)S(1)}, bf16[320,256]{1,0:T(8,128)(2,1)S(1)}, u32[]{:S(2)}, u32[]{:S(2)}) collective-permute-start(bf16[320,256]{1,0:T(8,128)(2,1)S(1)} %get-tuple-element.29.refs_0_.refs_1_), channel_id=1, source_target_pairs={{0,1},{1,0},{2,3},{3,2},{4,5},{5,4},{6,7},{7,6},{8,9},{9,8},{10,11... | collective-permute-start | bytes 491528 | tf_op jit(solution)/shard_map/ppermute | solution.py:495
  30.3 1.5 %collective-permute-start.9 = (bf16[320,256]{1,0:T(8,128)(2,1)S(1)}, bf16[320,256]{1,0:T(8,128)(2,1)S(1)}, u32[]{:S(2)}, u32[]{:S(2)}) collective-permute-start(bf16[320,256]{1,0:T(8,128)(2,1)S(1)} %collective-permute-done.7.refs_1_.refs_2_), channel_id=1, source_target_pairs={{0,1},{1,0},{2,3},{3,2},{4,5},{5,4},{6,7},{7,6},{8,9},{9,8},{10,11... | collective-permute-start | bytes 491528 | tf_op jit(solution)/shard_map/ppermute | solution.py:495
  30.3 15.4 %collective-permute-start.10 = (bf16[384,256]{1,0:T(8,128)(2,1)S(1)}, bf16[384,256]{1,0:T(8,128)(2,1)S(1)}, u32[]{:S(2)}, u32[]{:S(2)}) collective-permute-start(bf16[384,256]{1,0:T(8,128)(2,1)S(1)} %get-tuple-element.36.refs_5_), channel_id=1, source_target_pairs={{0,2},{1,3},{2,0},{3,1},{4,6},{5,7},{6,4},{7,5},{8,10},{9,11},{10,... | collective-permute-start | bytes 589832 | tf_op jit(solution)/shard_map/ppermute | solution.py:495
  31.8 23.3 %collective-permute-start.14 = (bf16[64,4096]{1,0:T(8,128)(2,1)}, bf16[64,4096]{1,0:T(8,128)(2,1)S(1)}, u32[]{:S(2)}, u32[]{:S(2)}) collective-permute-start(bf16[64,4096]{1,0:T(8,128)(2,1)} %get-tuple-element.45.refs_6_), channel_id=1, source_target_pairs={{0,2},{1,3},{2,0},{3,1},{4,6},{5,7},{6,4},{7,5},{8,10},{9,11},{10,... | collective-permute-start | bytes 1572872 | tf_op jit(solution)/shard_map/ppermute | solution.py:495
  37.2 17.9 %copy-start.1 = (bf16[64,4096]{1,0:T(8,128)(2,1)S(1)}, bf16[64,4096]{1,0:T(8,128)(2,1)}, u32[]{:S(2)}) copy-start(bf16[64,4096]{1,0:T(8,128)(2,1)} %get-tuple-element.45.refs_6_) | copy-start | bytes 1572868
  45.8 4.2 %collective-permute-start.12 = (bf16[384,256]{1,0:T(8,128)(2,1)S(1)}, bf16[384,256]{1,0:T(8,128)(2,1)S(1)}, u32[]{:S(2)}, u32[]{:S(2)}) collective-permute-start(bf16[384,256]{1,0:T(8,128)(2,1)S(1)} %get-tuple-element.36.refs_5_), channel_id=1, source_target_pairs={{0,1},{1,0},{2,3},{3,2},{4,5},{5,4},{6,7},{7,6},{8,9},{9,8},{10,11... | collective-permute-start | bytes 589832 | tf_op jit(solution)/shard_map/ppermute | solution.py:495
  45.8 4.2 %collective-permute-start.13 = (bf16[384,256]{1,0:T(8,128)(2,1)S(1)}, bf16[384,256]{1,0:T(8,128)(2,1)S(1)}, u32[]{:S(2)}, u32[]{:S(2)}) collective-permute-start(bf16[384,256]{1,0:T(8,128)(2,1)S(1)} %collective-permute-done.10.refs_6_), channel_id=1, source_target_pairs={{0,1},{1,0},{2,3},{3,2},{4,5},{5,4},{6,7},{7,6},{8,9},{9,8},{10,11... | collective-permute-start | bytes 589832 | tf_op jit(solution)/shard_map/ppermute | solution.py:495
  46.3 13.4 %collective-permute-start.15 = (bf16[64,4096]{1,0:T(8,128)(2,1)S(1)}, bf16[64,4096]{1,0:T(8,128)(2,1)S(1)}, u32[]{:S(2)}, u32[]{:S(2)}) collective-permute-start(bf16[64,4096]{1,0:T(8,128)(2,1)S(1)} %copy-done), channel_id=1, source_target_pairs={{0,1},{1,0},{2,3},{3,2},{4,5},{5,4},{6,7},{7,6},{8,9},{9,8},{10,11... | collective-permute-start | bytes 1572872 | tf_op jit(solution)/shard_map/ppermute | solution.py:495
  46.3 13.4 %collective-permute-start.16 = (bf16[64,4096]{1,0:T(8,128)(2,1)S(1)}, bf16[64,4096]{1,0:T(8,128)(2,1)S(1)}, u32[]{:S(2)}, u32[]{:S(2)}) collective-permute-start(bf16[64,4096]{1,0:T(8,128)(2,1)S(1)} %collective-permute-done.11.refs_3_), channel_id=1, source_target_pairs={{0,1},{1,0},{2,3},{3,2},{4,5},{5,4},{6,7},{7,6},{8,9},{9,8},{10,11... | collective-permute-start | bytes 1572872 | tf_op jit(solution)/shard_map/ppermute | solution.py:495
  50.0 9.8 %slice-start = ((s8[8388608]{0:T(1024)(128)(4,1)}), s8[4194304]{0:T(1024)(128)(4,1)S(1)}, s32[]{:S(2)}) async-start(s8[8388608]{0:T(1024)(128)(4,1)} %bitcast.1), calls=%async_computation | async-start | bytes 8388608
  55.1 4.7 %slice-start.1 = ((s8[8388608]{0:T(1024)(128)(4,1)}), s8[4194304]{0:T(1024)(128)(4,1)S(1)}, s32[]{:S(2)}) async-start(s8[8388608]{0:T(1024)(128)(4,1)} %bitcast.1), calls=%async_computation.1 | async-start | bytes 8388608
  55.1 4.6 %collective-permute-start.17 = (bf16[64,4096]{1,0:T(8,128)(2,1)S(1)}, bf16[64,4096]{1,0:T(8,128)(2,1)S(1)}, u32[]{:S(2)}, u32[]{:S(2)}) collective-permute-start(bf16[64,4096]{1,0:T(8,128)(2,1)S(1)} %copy-done.1), channel_id=1, source_target_pairs={{0,1},{1,0},{2,3},{3,2},{4,5},{5,4},{6,7},{7,6},{8,9},{9,8},{10,11... | collective-permute-start | bytes 1572872 | tf_op jit(solution)/shard_map/ppermute | solution.py:495
  55.1 4.6 %collective-permute-start.18 = (bf16[64,4096]{1,0:T(8,128)(2,1)S(1)}, bf16[64,4096]{1,0:T(8,128)(2,1)S(1)}, u32[]{:S(2)}, u32[]{:S(2)}) collective-permute-start(bf16[64,4096]{1,0:T(8,128)(2,1)S(1)} %collective-permute-done.14.refs_7_), channel_id=1, source_target_pairs={{0,1},{1,0},{2,3},{3,2},{4,5},{5,4},{6,7},{7,6},{8,9},{9,8},{10,11... | collective-permute-start | bytes 1572872 | tf_op jit(solution)/shard_map/ppermute | solution.py:495
  (1 other events, 0.9 us)
where the time goes:
time: 66.9 us; the launch traced here: 66.7 us
  Pallas kernels  28.9 us (43%)
  waiting for transfers between devices  18.5 us (28%)
  starting transfers between devices  18.1 us (27%)
  local copies, waits for them, and re-layouts  0.91 us (1%)
    ppermute x19, waiting for transfers between devices, swap(): return lax.ppermute(x, axis, [(i, i ^ mask) for i in range(size)])  18.5 us
    ppermute x19, starting transfers between devices, swap(): return lax.ppermute(x, axis, [(i, i ^ mask) for i in range(size)])  18.1 us
    pallas_call x1, Pallas kernels, finish(): pl.pallas_call(functools.partial(finish_kernel, apart), out_shape=jax.Sha...  6.79 us
    pallas_call x1, Pallas kernels, select(): pl.pallas_call(functools.partial(select_kernel, slot_count), out_shape=ou...  4.99 us
    pallas_call x1, Pallas kernels, third_half(): pl.pallas_call(functools.partial(third_kernel, apart, part), out_shape=[j...  4.73 us
    pallas_call x1, Pallas kernels, fourth_half(): pl.pallas_call(functools.partial(fourth_kernel, block_cols), out_shape=ja...  4.08 us
    pallas_call x1, Pallas kernels, first_half(): pl.pallas_call(functools.partial(first_kernel, apart, part), out_shape=ja...  3.95 us
    pallas_call x1, Pallas kernels, second_half(): pl.pallas_call(second_kernel, out_shape=jax.ShapeDtypeStruct(work.shape,...  3.18 us
  transfers between devices with their start and end apart: 19, of which 9 were waited for; matrix products, arithmetic and copies ran while one was open for 0% of the time, Pallas kernels for 24%

commit v1 on v0

--- a/solution.py
+++ b/solution.py
@@ -10,11 +10,11 @@
 LANES = 128
 LEAF = 32
 SUB = 16
-CHUNK = 512
-SELECT = 1024
+CHUNK = 1024
+SELECT = 512
 MICRO = 1 << 29
 MIB = 1 << 20
-ALMOST_ALL = 63 * MIB
+ALMOST_ALL = 52 * MIB
 
 
 def masks_of(size):
@@ -69,9 +69,11 @@
 def select_kernel(slot_count, pivots_ref, vectors_ref, integrals_ref, *refs):
     panels, block_cols, _ = integrals_ref.shape
     found_ref, out_refs = refs[0], refs[1 : 1 + panels]
-    vec, ints, sems = refs[1 + panels :]
+    vec, ints, local_pivots, sems = refs[1 + panels :]
     part, row_count = vec.shape
     width = pivots_ref.shape[1]
+    listed = pltpu.make_async_copy(pivots_ref, local_pivots, sems.at[sems.shape[0] - 1])
+    listed.start()
     lanes = panels * slot_count
     first = pl.multiple_of(lax.axis_index("cols") * part, part)
     step = min(SELECT, row_count)
@@ -87,11 +89,12 @@
     whole = pltpu.make_async_copy(integrals_ref, ints, sems.at[count])
     for copy in copies[:1] + [whole] + copies[1:]:
         copy.start()
+    listed.wait()
     start = (lax.axis_index("rows") * row_count).astype(jnp.float32)
     square = (width, width)
     target = jnp.zeros((1, lanes), jnp.float32)
     for panel in range(panels):
-        local = pivots_ref[panel : panel + 1, :].astype(jnp.float32) - start
+        local = local_pivots[panel : panel + 1, :].astype(jnp.float32) - start
         mine = ((local >= 0.0) & (local < row_count)).astype(jnp.float32)
         earlier = iota(square, 1) < iota(square, 0)
         rank = jnp.sum(
@@ -130,17 +133,14 @@
     results = pl.pallas_call(
         functools.partial(select_kernel, slot_count),
         out_shape=outs,
-        in_specs=[
-            pl.BlockSpec(memory_space=pltpu.VMEM),
-            pl.BlockSpec(memory_space=pltpu.HBM),
-            pl.BlockSpec(memory_space=pltpu.HBM),
-        ],
+        in_specs=[pl.BlockSpec(memory_space=pl.ANY)] * 3,
         out_specs=[pl.BlockSpec(memory_space=pltpu.VMEM)]
         + [pl.BlockSpec(memory_space=pltpu.HBM)] * panels,
         scratch_shapes=[
             pltpu.VMEM((part, row_count), jnp.bfloat16),
             pltpu.VMEM(integrals.shape, jnp.bfloat16),
-            pltpu.SemaphoreType.DMA((row_count // min(SELECT, row_count) + 1 + panels,)),
+            pltpu.VMEM(pivots.shape, jnp.int32),
+            pltpu.SemaphoreType.DMA((row_count // min(SELECT, row_count) + 2 + panels,)),
         ],
         compiler_params=pltpu.CompilerParams(vmem_limit_bytes=ALMOST_ALL),
         cost_estimate=pl.CostEstimate(flops=MICRO * 2, bytes_accessed=3 * MIB, transcendentals=0),
@@ -427,27 +427,18 @@
     count = len(apart)
     left, vectors_ref = refs[0], refs[1]
     blocks = refs[2 : 2 + 2 * count]
-    out_ref, right, result, sems, out_sems = refs[2 + 2 * count :]
+    out_ref, right, result, out_sems = refs[2 + 2 * count :]
     me = lax.axis_index("cols")
     pairs = vectors_ref.shape[1]
     block_cols = blocks[0].shape[0]
     both = right.shape[0]
-    copies = []
+    outs = []
     for n in range(pairs // CHUNK):
+        at = slice(n * CHUNK, (n + 1) * CHUNK)
         for i, ref in enumerate(blocks):
             place = i // count * (both // 2) + (me ^ apart[i % count]) * block_cols
-            rows = pl.ds(pl.multiple_of(place, block_cols), block_cols)
-            at = pl.ds(n * CHUNK, CHUNK)
-            copies.append(
-                pltpu.make_async_copy(ref.at[:, at], right.at[rows, at], sems.at[n, i])
-            )
-            copies[-1].start()
-    outs = []
-    for n in range(pairs // CHUNK):
-        at = pl.ds(n * CHUNK, CHUNK)
-        for copy in copies[n * len(blocks) : (n + 1) * len(blocks)]:
-            copy.wait()
-        halves = dot(left[:, both:], vectors_ref[:, at]) + dot(left[:, :both], right[:, at])
+            right[pl.ds(pl.multiple_of(place, block_cols), block_cols), :] = ref[:, at]
+        halves = dot(left[:, both:], vectors_ref[:, at]) + dot(left[:, :both], right[...])
         value = halves[: 2 * block_cols] + halves[2 * block_cols :]
         result[0, :, at] = value[:block_cols]
         result[1, :, at] = value[block_cols:]
@@ -465,13 +456,11 @@
     return pl.pallas_call(
         functools.partial(finish_kernel, apart),
         out_shape=jax.ShapeDtypeStruct((2, block_cols, pairs), jnp.float32),
-        in_specs=[pl.BlockSpec(memory_space=pltpu.VMEM)] * 2
-        + [pl.BlockSpec(memory_space=pl.ANY)] * len(blocks),
+        in_specs=[pl.BlockSpec(memory_space=pltpu.VMEM)] * (2 + len(blocks)),
         out_specs=pl.BlockSpec(memory_space=pl.ANY),
         scratch_shapes=[
-            pltpu.VMEM((both, pairs), jnp.bfloat16),
+            pltpu.VMEM((both, CHUNK), jnp.bfloat16),
             pltpu.VMEM((2, block_cols, pairs), jnp.float32),
-            pltpu.SemaphoreType.DMA((pairs // CHUNK, len(blocks))),
             pltpu.SemaphoreType.DMA((pairs // CHUNK,)),
         ],
         compiler_params=pltpu.CompilerParams(vmem_limit_bytes=24 * MIB),
@@ -519,18 +508,19 @@
     far0 = swap(ints[0], "cols", far_mask)
     other0 = swap(own0, "cols", far_mask)
     other1 = swap(own1, "cols", far_mask)
-    pair1 = [own1, other1]
     picked0 = [own0, other0] + near([own0]) + near([other0])
+    beside1 = near([own1])
+    beside = near(ints)
     picked0, last = lax.optimization_barrier((picked0, ints[1]))
     far1 = swap(last, "cols", far_mask)
     work0 = first_half(picked0, apart, part)
-    work0, pair1, ints0 = lax.optimization_barrier((work0, pair1, [ints[0], far0]))
-    picked1 = pair1 + near(pair1)
-    blocks = ints0 + near(ints0)
+    work0, other1, far0 = lax.optimization_barrier((work0, other1, far0))
+    picked1 = [own1, other1] + beside1 + near([other1])
+    blocks = [ints[0], far0, beside[0]] + near([far0])
     work0 = second_half(work0)
     work1, rows_of, ahead = third_half(work0, picked0, picked1, apart, part)
-    work1, ints1 = lax.optimization_barrier((work1, [last, far1]))
-    blocks += ints1 + near(ints1)
+    work1, far1 = lax.optimization_barrier((work1, far1))
+    blocks += [last, far1, beside[1]] + near([far1])
     left = fourth_half(work0, work1, rows_of, ahead, block_cols)
     return finish(left, vectors, blocks, apart)
 

time: 66.9 us -> 62 us (0.927)
  Pallas kernels: 28.9 us -> 25.1 us
  starting transfers between devices: 18.1 us -> 17.1 us
    pallas_call x1, Pallas kernels: 6.79 us -> 4.43 us  [finish(): pl.pallas_call(functools.partial(finish_kernel, apart), out_shape=jax.Sha...]
    pallas_call x1, Pallas kernels: 4.99 us -> 3.72 us  [select(): pl.pallas_call(functools.partial(select_kernel, slot_count), out_shape=ou...]
    ppermute x19, starting transfers between devices: 18.1 us -> 17.1 us  [swap(): return lax.ppermute(x, axis, [(i, i ^ mask) for i in range(size)])]
  transfers between devices with their start and end apart: 19 -> 19, of which waited for: 9 -> 9; matrix products, arithmetic and copies ran while one was open for 0% -> 0% of each run, Pallas kernels for 24% -> 26%
where the time goes in v1:
time: 62 us; the launch traced here: 61.8 us
  Pallas kernels  25.1 us (40%)
  waiting for transfers between devices  18.6 us (30%)
  starting transfers between devices  17.1 us (28%)
  local copies, waits for them, and re-layouts  0.69 us (1%)
    ppermute x19, waiting for transfers between devices, swap(): return lax.ppermute(x, axis, [(i, i ^ mask) for i in range(size)])  18.6 us
    ppermute x19, starting transfers between devices, swap(): return lax.ppermute(x, axis, [(i, i ^ mask) for i in range(size)])  17.1 us
    pallas_call x1, Pallas kernels, third_half(): pl.pallas_call(functools.partial(third_kernel, apart, part), out_shape=[j...  4.73 us
    pallas_call x1, Pallas kernels, finish(): pl.pallas_call(functools.partial(finish_kernel, apart), out_shape=jax.Sha...  4.43 us
    pallas_call x1, Pallas kernels, fourth_half(): pl.pallas_call(functools.partial(fourth_kernel, block_cols), out_shape=ja...  3.97 us
    pallas_call x1, Pallas kernels, first_half(): pl.pallas_call(functools.partial(first_kernel, apart, part), out_shape=ja...  3.95 us
    pallas_call x1, Pallas kernels, select(): pl.pallas_call(functools.partial(select_kernel, slot_count), out_shape=ou...  3.72 us
    pallas_call x1, Pallas kernels, second_half(): pl.pallas_call(second_kernel, out_shape=jax.ShapeDtypeStruct(work.shape,...  3.18 us
  transfers between devices with their start and end apart: 19, of which 9 were waited for; matrix products, arithmetic and copies ran while one was open for 0% of the time, Pallas kernels for 26%

profile of v1, /device:TPU:0, one launch (start us, length us, event | category | flops | bytes accessed | tf_op | source)
XLA Modules:
  0.0 61.8 jit_solution(2560573476558532509)
XLA Ops:
  0.0 0.7 %copy-done = s32[2,256]{1,0:T(2,128)S(1)} copy-done((s32[2,256]{1,0:T(2,128)S(1)}, s32[2,256]{1,0:T(2,128)}, u32[]{:S(2)}) %copy-start) | copy-done | bytes 2072
  0.7 3.7 %select.1 = (bf16[352,128]{1,0:T(8,128)(2,1)S(1)}, bf16[64,4096]{1,0:T(8,128)(2,1)S(1)}, bf16[64,4096]{1,0:T(8,128)(2,1)S(1)}) custom-call(s32[2,256]{1,0:T(2,128)S(1)} %copy-done, bf16[1024,4096]{1,0:T(8,128)(2,1)} %refs_1_.1, bf16[2,64,4096]{2,1,0:T(8,128)(2,1)} %integrals_ref.1), custom_call_target="tpu_custom_call" | custom-call | flops 1073741824 | bytes 3145728 | tf_op jit(solution)/shard_map/select/pallas_call | solution.py:133
  4.4 4.1 %collective-permute-start = (bf16[1,352,128]{2,1,0:T(8,128)(2,1)S(1)}, bf16[1,352,128]{2,1,0:T(8,128)(2,1)S(1)}, u32[]{:S(2)}, u32[]{:S(2)}) collective-permute-start(bf16[1,352,128]{2,1,0:T(8,128)(2,1)S(1)} %bitcast.3), channel_id=1, source_target_pairs={{0,16},{4,20},{8,24},{12,28},{16,0},{20,4},{24,8},{28,12},{1,17},{... | collective-permute-start | bytes 270344 | tf_op jit(solution)/shard_map/ppermute | solution.py:484
  8.5 2.5 %collective-permute-start.5 = (bf16[1,352,128]{2,1,0:T(8,128)(2,1)S(1)}, bf16[1,352,128]{2,1,0:T(8,128)(2,1)S(1)}, u32[]{:S(2)}, u32[]{:S(2)}) collective-permute-start(bf16[1,352,128]{2,1,0:T(8,128)(2,1)S(1)} %bitcast.4), channel_id=1, source_target_pairs={{0,12},{4,8},{8,4},{12,0},{16,28},{20,24},{24,20},{28,16},{1,13},{... | collective-permute-start | bytes 270344 | tf_op jit(solution)/shard_map/ppermute | solution.py:484
  11.0 0.5 collective-permute-start.3
  12.0 0.8 %collective-permute-done.refs_1_ = bf16[1,352,128]{2,1,0:T(8,128)(2,1)S(1)} collective-permute-done((bf16[1,352,128]{2,1,0:T(8,128)(2,1)S(1)}, bf16[1,352,128]{2,1,0:T(8,128)(2,1)S(1)}, u32[]{:S(2)}, u32[]{:S(2)}) %collective-permute-start) | collective-permute-done | bytes 90144 | tf_op jit(solution)/shard_map/ppermute | solution.py:484
  12.8 2.0 %collective-permute-start.6 = (bf16[1,352,128]{2,1,0:T(8,128)(2,1)S(1)}, bf16[1,352,128]{2,1,0:T(8,128)(2,1)S(1)}, u32[]{:S(2)}, u32[]{:S(2)}) collective-permute-start(bf16[1,352,128]{2,1,0:T(8,128)(2,1)S(1)} %collective-permute-done.refs_1_), channel_id=1, source_target_pairs={{0,12},{4,8},{8,4},{12,0},{16,28},{20,24},{24,20},{28,16},{1,13},{... | collective-permute-start | bytes 270344 | tf_op jit(solution)/shard_map/ppermute | solution.py:484
  14.8 0.5 collective-permute-start.4
  15.4 1.4 %collective-permute-start.2 = (bf16[1,352,128]{2,1,0:T(8,128)(2,1)S(1)}, bf16[1,352,128]{2,1,0:T(8,128)(2,1)S(1)}, u32[]{:S(2)}, u32[]{:S(2)}) collective-permute-start(bf16[1,352,128]{2,1,0:T(8,128)(2,1)S(1)} %collective-permute-done.refs_1_), channel_id=1, source_target_pairs={{0,8},{4,12},{8,0},{12,4},{16,24},{20,28},{24,16},{28,20},{1,9},{5... | collective-permute-start | bytes 270344 | tf_op jit(solution)/shard_map/ppermute | solution.py:484
  17.0 1.6 %collective-permute-done.6.refs_7_ = bf16[1,352,128]{2,1,0:T(8,128)(2,1)S(1)} collective-permute-done((bf16[1,352,128]{2,1,0:T(8,128)(2,1)S(1)}, bf16[1,352,128]{2,1,0:T(8,128)(2,1)S(1)}, u32[]{:S(2)}, u32[]{:S(2)}) %collective-permute-start.6) | collective-permute-done | bytes 90144 | tf_op jit(solution)/shard_map/ppermute | solution.py:484
  18.6 1.1 %collective-permute-done.4.refs_5_ = bf16[1,352,128]{2,1,0:T(8,128)(2,1)S(1)} collective-permute-done((bf16[1,352,128]{2,1,0:T(8,128)(2,1)S(1)}, bf16[1,352,128]{2,1,0:T(8,128)(2,1)S(1)}, u32[]{:S(2)}, u32[]{:S(2)}) %collective-permute-start.4) | collective-permute-done | bytes 90144 | tf_op jit(solution)/shard_map/ppermute | solution.py:484
  20.2 1.2 %compact.1 = (bf16[320,256]{1,0:T(8,128)(2,1)S(1)}, bf16[384,256]{1,0:T(8,128)(2,1)S(1)}) custom-call(s32[2,256]{1,0:T(2,128)S(1)} %copy-done, bf16[1,352,128]{2,1,0:T(8,128)(2,1)S(1)} %bitcast.7, bf16[1,352,128]{2,1,0:T(8,128)(2,1)S(1)} %collective-permute-done.refs_1_, bf16[1,352,128]{2,1,0:T(8,128)(2,1)S(1)} %collective-permute-done.1.refs_2_, ...), custom_call_target="tpu_custom_call" | custom-call | flops 536870912 | bytes 1048576 | tf_op jit(solution)/shard_map/compact/pallas_call | solution.py:195
  21.4 1.6 %collective-permute-start.7 = (bf16[320,256]{1,0:T(8,128)(2,1)S(1)}, bf16[320,256]{1,0:T(8,128)(2,1)S(1)}, u32[]{:S(2)}, u32[]{:S(2)}) collective-permute-start(bf16[320,256]{1,0:T(8,128)(2,1)S(1)} %get-tuple-element.26.refs_0_.refs_1_), channel_id=1, source_target_pairs={{0,2},{1,3},{2,0},{3,1},{4,6},{5,7},{6,4},{7,5},{8,10},{9,11},{10,... | collective-permute-start | bytes 491528 | tf_op jit(solution)/shard_map/ppermute | solution.py:484
  23.4 5.0 %collective-permute-done.7.refs_1_.refs_2_ = bf16[320,256]{1,0:T(8,128)(2,1)S(1)} collective-permute-done((bf16[320,256]{1,0:T(8,128)(2,1)S(1)}, bf16[320,256]{1,0:T(8,128)(2,1)S(1)}, u32[]{:S(2)}, u32[]{:S(2)}) %collective-permute-start.7) | collective-permute-done | bytes 163872 | tf_op jit(solution)/shard_map/ppermute | solution.py:484
  29.0 1.5 %collective-permute-start.10 = (bf16[384,256]{1,0:T(8,128)(2,1)S(1)}, bf16[384,256]{1,0:T(8,128)(2,1)S(1)}, u32[]{:S(2)}, u32[]{:S(2)}) collective-permute-start(bf16[384,256]{1,0:T(8,128)(2,1)S(1)} %get-tuple-element.30.refs_5_), channel_id=1, source_target_pairs={{0,2},{1,3},{2,0},{3,1},{4,6},{5,7},{6,4},{7,5},{8,10},{9,11},{10,... | collective-permute-start | bytes 589832 | tf_op jit(solution)/shard_map/ppermute | solution.py:484
  30.5 0.9 %collective-permute-start.14 = (bf16[64,4096]{1,0:T(8,128)(2,1)S(1)}, bf16[64,4096]{1,0:T(8,128)(2,1)S(1)}, u32[]{:S(2)}, u32[]{:S(2)}) collective-permute-start(bf16[64,4096]{1,0:T(8,128)(2,1)S(1)} %get-tuple-element.35.refs_6_), channel_id=1, source_target_pairs={{0,2},{1,3},{2,0},{3,1},{4,6},{5,7},{6,4},{7,5},{8,10},{9,11},{10,... | collective-permute-start | bytes 1572872 | tf_op jit(solution)/shard_map/ppermute | solution.py:484
  31.4 3.9 %first_half.1.before_ref = f32[256,512]{1,0:T(8,128)S(1)} custom-call(bf16[320,256]{1,0:T(8,128)(2,1)S(1)} %get-tuple-element.26.refs_0_.refs_1_, bf16[320,256]{1,0:T(8,128)(2,1)S(1)} %collective-permute-done.7.refs_1_.refs_2_, bf16[320,256]{1,0:T(8,128)(2,1)S(1)} %collective-permute-done.8.refs_2_.refs_3_, ...), custom_call_target="tpu_custom_call" | custom-call | flops 2147483648 | bytes 1048576 | tf_op jit(solution)/shard_map/first_half/pallas_call | solution.py:317
  35.4 8.6 %collective-permute-done.10.refs_6_ = bf16[384,256]{1,0:T(8,128)(2,1)S(1)} collective-permute-done((bf16[384,256]{1,0:T(8,128)(2,1)S(1)}, bf16[384,256]{1,0:T(8,128)(2,1)S(1)}, u32[]{:S(2)}, u32[]{:S(2)}) %collective-permute-start.10) | collective-permute-done | bytes 196640 | tf_op jit(solution)/shard_map/ppermute | solution.py:484
  43.9 0.5 collective-permute-start.13
  44.5 3.2 %second_half.1.refs_0_.work0 = f32[256,512]{1,0:T(8,128)S(1)} custom-call(f32[256,512]{1,0:T(8,128)S(1)} %first_half.1.before_ref), custom_call_target="tpu_custom_call" | custom-call | flops 2147483648 | bytes 1048576 | tf_op jit(solution)/shard_map/second_half/pallas_call | solution.py:338
  47.7 4.7 %third_half.1 = (f32[256,512]{1,0:T(8,128)S(1)}, bf16[1024,512]{1,0:T(8,128)(2,1)S(1)}, bf16[256,256]{1,0:T(8,128)(2,1)S(1)}) custom-call(f32[256,512]{1,0:T(8,128)S(1)} %second_half.1.refs_0_.work0, bf16[320,256]{1,0:T(8,128)(2,1)S(1)} %get-tuple-element.26.refs_0_.refs_1_, bf16[320,256]{1,0:T(8,128)(2,1)S(1)} %collective-permute-done.7.refs_1_.refs_2_, ...), custom_call_target="tpu_custom_call" | custom-call | flops 2684354560 | bytes 1048576 | tf_op jit(solution)/shard_map/third_half/pallas_call | solution.py:373
  52.5 0.7 %collective-permute-done.14.refs_7_ = bf16[64,4096]{1,0:T(8,128)(2,1)S(1)} collective-permute-done((bf16[64,4096]{1,0:T(8,128)(2,1)S(1)}, bf16[64,4096]{1,0:T(8,128)(2,1)S(1)}, u32[]{:S(2)}, u32[]{:S(2)}) %collective-permute-start.14) | collective-permute-done | bytes 524320 | tf_op jit(solution)/shard_map/ppermute | solution.py:484
  53.2 4.0 %fourth_half.1.refs_0_ = bf16[256,1536]{1,0:T(8,128)(2,1)S(1)} custom-call(f32[256,512]{1,0:T(8,128)S(1)} %second_half.1.refs_0_.work0, f32[256,512]{1,0:T(8,128)S(1)} %get-tuple-element.36.before_ref, bf16[1024,512]{1,0:T(8,128)(2,1)S(1)} %get-tuple-element.37.rows_of, bf16[256,256]{1,0:T(8,128)(2,1)S(1)} %get-tuple-element.38.ahead), custom_call_target="tpu_custom_call" | custom-call | flops 2684354560 | bytes 1048576 | tf_op jit(solution)/shard_map/fourth_half/pallas_call | solution.py:412
  57.2 4.4 %finish.1 = f32[2,64,4096]{2,1,0:T(8,128)} custom-call(bf16[256,1536]{1,0:T(8,128)(2,1)S(1)} %fourth_half.1.refs_0_, bf16[1024,4096]{1,0:T(8,128)(2,1)S(1)} %bitcast.2, bf16[64,4096]{1,0:T(8,128)(2,1)S(1)} %get-tuple-element.31.refs_2_, bf16[64,4096]{1,0:T(8,128)(2,1)S(1)} %collective-permute-done.11.refs_3_, ...), custom_call_target="tpu_custom_call" | custom-call | flops 3221225472 | bytes 16777216 | tf_op jit(solution)/shard_map/finish/pallas_call | solution.py:456
  (28 shorter events, 2.3 us)
Async XLA Ops:
  0.0 0.7 %copy-start = (s32[2,256]{1,0:T(2,128)S(1)}, s32[2,256]{1,0:T(2,128)}, u32[]{:S(2)}) copy-start(s32[2,256]{1,0:T(2,128)} %pivots_ref.3) | copy-start | bytes 6148
  4.4 8.4 %collective-permute-start = (bf16[1,352,128]{2,1,0:T(8,128)(2,1)S(1)}, bf16[1,352,128]{2,1,0:T(8,128)(2,1)S(1)}, u32[]{:S(2)}, u32[]{:S(2)}) collective-permute-start(bf16[1,352,128]{2,1,0:T(8,128)(2,1)S(1)} %bitcast.3), channel_id=1, source_target_pairs={{0,16},{4,20},{8,24},{12,28},{16,0},{20,4},{24,8},{28,12},{1,17},{... | collective-permute-start | bytes 270344 | tf_op jit(solution)/shard_map/ppermute | solution.py:484
  8.5 6.8 %collective-permute-start.5 = (bf16[1,352,128]{2,1,0:T(8,128)(2,1)S(1)}, bf16[1,352,128]{2,1,0:T(8,128)(2,1)S(1)}, u32[]{:S(2)}, u32[]{:S(2)}) collective-permute-start(bf16[1,352,128]{2,1,0:T(8,128)(2,1)S(1)} %bitcast.4), channel_id=1, source_target_pairs={{0,12},{4,8},{8,4},{12,0},{16,28},{20,24},{24,20},{28,16},{1,13},{... | collective-permute-start | bytes 270344 | tf_op jit(solution)/shard_map/ppermute | solution.py:484
  11.0 5.8 %collective-permute-start.3 = (bf16[1,352,128]{2,1,0:T(8,128)(2,1)S(1)}, bf16[1,352,128]{2,1,0:T(8,128)(2,1)S(1)}, u32[]{:S(2)}, u32[]{:S(2)}) collective-permute-start(bf16[1,352,128]{2,1,0:T(8,128)(2,1)S(1)} %bitcast.5), channel_id=1, source_target_pairs={{0,4},{4,0},{8,12},{12,8},{16,20},{20,16},{24,28},{28,24},{1,5},{5... | collective-permute-start | bytes 270344 | tf_op jit(solution)/shard_map/ppermute | solution.py:484
  11.6 5.5 %collective-permute-start.1 = (bf16[1,352,128]{2,1,0:T(8,128)(2,1)S(1)}, bf16[1,352,128]{2,1,0:T(8,128)(2,1)S(1)}, u32[]{:S(2)}, u32[]{:S(2)}) collective-permute-start(bf16[1,352,128]{2,1,0:T(8,128)(2,1)S(1)} %bitcast.6), channel_id=1, source_target_pairs={{0,8},{4,12},{8,0},{12,4},{16,24},{20,28},{24,16},{28,20},{1,9},{5... | collective-permute-start | bytes 270344 | tf_op jit(solution)/shard_map/ppermute | solution.py:484
  12.8 5.8 %collective-permute-start.6 = (bf16[1,352,128]{2,1,0:T(8,128)(2,1)S(1)}, bf16[1,352,128]{2,1,0:T(8,128)(2,1)S(1)}, u32[]{:S(2)}, u32[]{:S(2)}) collective-permute-start(bf16[1,352,128]{2,1,0:T(8,128)(2,1)S(1)} %collective-permute-done.refs_1_), channel_id=1, source_target_pairs={{0,12},{4,8},{8,4},{12,0},{16,28},{20,24},{24,20},{28,16},{1,13},{... | collective-permute-start | bytes 270344 | tf_op jit(solution)/shard_map/ppermute | solution.py:484
  14.8 4.9 %collective-permute-start.4 = (bf16[1,352,128]{2,1,0:T(8,128)(2,1)S(1)}, bf16[1,352,128]{2,1,0:T(8,128)(2,1)S(1)}, u32[]{:S(2)}, u32[]{:S(2)}) collective-permute-start(bf16[1,352,128]{2,1,0:T(8,128)(2,1)S(1)} %collective-permute-done.refs_1_), channel_id=1, source_target_pairs={{0,4},{4,0},{8,12},{12,8},{16,20},{20,16},{24,28},{28,24},{1,5},{5... | collective-permute-start | bytes 270344 | tf_op jit(solution)/shard_map/ppermute | solution.py:484
  15.4 4.8 %collective-permute-start.2 = (bf16[1,352,128]{2,1,0:T(8,128)(2,1)S(1)}, bf16[1,352,128]{2,1,0:T(8,128)(2,1)S(1)}, u32[]{:S(2)}, u32[]{:S(2)}) collective-permute-start(bf16[1,352,128]{2,1,0:T(8,128)(2,1)S(1)} %collective-permute-done.refs_1_), channel_id=1, source_target_pairs={{0,8},{4,12},{8,0},{12,4},{16,24},{20,28},{24,16},{28,20},{1,9},{5... | collective-permute-start | bytes 270344 | tf_op jit(solution)/shard_map/ppermute | solution.py:484
  21.4 7.1 %collective-permute-start.7 = (bf16[320,256]{1,0:T(8,128)(2,1)S(1)}, bf16[320,256]{1,0:T(8,128)(2,1)S(1)}, u32[]{:S(2)}, u32[]{:S(2)}) collective-permute-start(bf16[320,256]{1,0:T(8,128)(2,1)S(1)} %get-tuple-element.26.refs_0_.refs_1_), channel_id=1, source_target_pairs={{0,2},{1,3},{2,0},{3,1},{4,6},{5,7},{6,4},{7,5},{8,10},{9,11},{10,... | collective-permute-start | bytes 491528 | tf_op jit(solution)/shard_map/ppermute | solution.py:484
  22.9 21.0 %collective-permute-start.11 = (bf16[64,4096]{1,0:T(8,128)(2,1)S(1)}, bf16[64,4096]{1,0:T(8,128)(2,1)S(1)}, u32[]{:S(2)}, u32[]{:S(2)}) collective-permute-start(bf16[64,4096]{1,0:T(8,128)(2,1)S(1)} %get-tuple-element.31.refs_2_), channel_id=1, source_target_pairs={{0,2},{1,3},{2,0},{3,1},{4,6},{5,7},{6,4},{7,5},{8,10},{9,11},{10,... | collective-permute-start | bytes 1572872 | tf_op jit(solution)/shard_map/ppermute | solution.py:484
  23.4 5.6 %collective-permute-start.8 = (bf16[320,256]{1,0:T(8,128)(2,1)S(1)}, bf16[320,256]{1,0:T(8,128)(2,1)S(1)}, u32[]{:S(2)}, u32[]{:S(2)}) collective-permute-start(bf16[320,256]{1,0:T(8,128)(2,1)S(1)} %get-tuple-element.26.refs_0_.refs_1_), channel_id=1, source_target_pairs={{0,1},{1,0},{2,3},{3,2},{4,5},{5,4},{6,7},{7,6},{8,9},{9,8},{10,11... | collective-permute-start | bytes 491528 | tf_op jit(solution)/shard_map/ppermute | solution.py:484
  28.5 2.0 %collective-permute-start.9 = (bf16[320,256]{1,0:T(8,128)(2,1)S(1)}, bf16[320,256]{1,0:T(8,128)(2,1)S(1)}, u32[]{:S(2)}, u32[]{:S(2)}) collective-permute-start(bf16[320,256]{1,0:T(8,128)(2,1)S(1)} %collective-permute-done.7.refs_1_.refs_2_), channel_id=1, source_target_pairs={{0,1},{1,0},{2,3},{3,2},{4,5},{5,4},{6,7},{7,6},{8,9},{9,8},{10,11... | collective-permute-start | bytes 491528 | tf_op jit(solution)/shard_map/ppermute | solution.py:484
  28.5 28.7 %collective-permute-start.15 = (bf16[64,4096]{1,0:T(8,128)(2,1)S(1)}, bf16[64,4096]{1,0:T(8,128)(2,1)S(1)}, u32[]{:S(2)}, u32[]{:S(2)}) collective-permute-start(bf16[64,4096]{1,0:T(8,128)(2,1)S(1)} %get-tuple-element.31.refs_2_), channel_id=1, source_target_pairs={{0,1},{1,0},{2,3},{3,2},{4,5},{5,4},{6,7},{7,6},{8,9},{9,8},{10,11... | collective-permute-start | bytes 1572872 | tf_op jit(solution)/shard_map/ppermute | solution.py:484
  29.0 28.2 %collective-permute-start.17 = (bf16[64,4096]{1,0:T(8,128)(2,1)S(1)}, bf16[64,4096]{1,0:T(8,128)(2,1)S(1)}, u32[]{:S(2)}, u32[]{:S(2)}) collective-permute-start(bf16[64,4096]{1,0:T(8,128)(2,1)S(1)} %get-tuple-element.35.refs_6_), channel_id=1, source_target_pairs={{0,1},{1,0},{2,3},{3,2},{4,5},{5,4},{6,7},{7,6},{8,9},{9,8},{10,11... | collective-permute-start | bytes 1572872 | tf_op jit(solution)/shard_map/ppermute | solution.py:484
  29.0 14.9 %collective-permute-start.10 = (bf16[384,256]{1,0:T(8,128)(2,1)S(1)}, bf16[384,256]{1,0:T(8,128)(2,1)S(1)}, u32[]{:S(2)}, u32[]{:S(2)}) collective-permute-start(bf16[384,256]{1,0:T(8,128)(2,1)S(1)} %get-tuple-element.30.refs_5_), channel_id=1, source_target_pairs={{0,2},{1,3},{2,0},{3,1},{4,6},{5,7},{6,4},{7,5},{8,10},{9,11},{10,... | collective-permute-start | bytes 589832 | tf_op jit(solution)/shard_map/ppermute | solution.py:484
  30.5 22.6 %collective-permute-start.14 = (bf16[64,4096]{1,0:T(8,128)(2,1)S(1)}, bf16[64,4096]{1,0:T(8,128)(2,1)S(1)}, u32[]{:S(2)}, u32[]{:S(2)}) collective-permute-start(bf16[64,4096]{1,0:T(8,128)(2,1)S(1)} %get-tuple-element.35.refs_6_), channel_id=1, source_target_pairs={{0,2},{1,3},{2,0},{3,1},{4,6},{5,7},{6,4},{7,5},{8,10},{9,11},{10,... | collective-permute-start | bytes 1572872 | tf_op jit(solution)/shard_map/ppermute | solution.py:484
  43.9 3.7 %collective-permute-start.12 = (bf16[384,256]{1,0:T(8,128)(2,1)S(1)}, bf16[384,256]{1,0:T(8,128)(2,1)S(1)}, u32[]{:S(2)}, u32[]{:S(2)}) collective-permute-start(bf16[384,256]{1,0:T(8,128)(2,1)S(1)} %get-tuple-element.30.refs_5_), channel_id=1, source_target_pairs={{0,1},{1,0},{2,3},{3,2},{4,5},{5,4},{6,7},{7,6},{8,9},{9,8},{10,11... | collective-permute-start | bytes 589832 | tf_op jit(solution)/shard_map/ppermute | solution.py:484
  43.9 3.8 %collective-permute-start.13 = (bf16[384,256]{1,0:T(8,128)(2,1)S(1)}, bf16[384,256]{1,0:T(8,128)(2,1)S(1)}, u32[]{:S(2)}, u32[]{:S(2)}) collective-permute-start(bf16[384,256]{1,0:T(8,128)(2,1)S(1)} %collective-permute-done.10.refs_6_), channel_id=1, source_target_pairs={{0,1},{1,0},{2,3},{3,2},{4,5},{5,4},{6,7},{7,6},{8,9},{9,8},{10,11... | collective-permute-start | bytes 589832 | tf_op jit(solution)/shard_map/ppermute | solution.py:484
  47.6 9.6 %slice-start = ((s8[8388608]{0:T(1024)(128)(4,1)}), s8[4194304]{0:T(1024)(128)(4,1)S(1)}, s32[]{:S(2)}) async-start(s8[8388608]{0:T(1024)(128)(4,1)} %bitcast.1), calls=%async_computation | async-start | bytes 8388608
  47.7 9.5 %collective-permute-start.16 = (bf16[64,4096]{1,0:T(8,128)(2,1)S(1)}, bf16[64,4096]{1,0:T(8,128)(2,1)S(1)}, u32[]{:S(2)}, u32[]{:S(2)}) collective-permute-start(bf16[64,4096]{1,0:T(8,128)(2,1)S(1)} %collective-permute-done.11.refs_3_), channel_id=1, source_target_pairs={{0,1},{1,0},{2,3},{3,2},{4,5},{5,4},{6,7},{7,6},{8,9},{9,8},{10,11... | collective-permute-start | bytes 1572872 | tf_op jit(solution)/shard_map/ppermute | solution.py:484
  53.2 4.0 %slice-start.1 = ((s8[8388608]{0:T(1024)(128)(4,1)}), s8[4194304]{0:T(1024)(128)(4,1)S(1)}, s32[]{:S(2)}) async-start(s8[8388608]{0:T(1024)(128)(4,1)} %bitcast.1), calls=%async_computation.1 | async-start | bytes 8388608
  53.2 4.0 %collective-permute-start.18 = (bf16[64,4096]{1,0:T(8,128)(2,1)S(1)}, bf16[64,4096]{1,0:T(8,128)(2,1)S(1)}, u32[]{:S(2)}, u32[]{:S(2)}) collective-permute-start(bf16[64,4096]{1,0:T(8,128)(2,1)S(1)} %collective-permute-done.14.refs_7_), channel_id=1, source_target_pairs={{0,1},{1,0},{2,3},{3,2},{4,5},{5,4},{6,7},{7,6},{8,9},{9,8},{10,11... | collective-permute-start | bytes 1572872 | tf_op jit(solution)/shard_map/ppermute | solution.py:484

commit v2 on v1

--- a/solution.py
+++ b/solution.py
@@ -10,7 +10,7 @@
 LANES = 128
 LEAF = 32
 SUB = 16
-CHUNK = 1024
+CHUNK = 512
 SELECT = 512
 MICRO = 1 << 29
 MIB = 1 << 20
@@ -149,11 +149,9 @@
     return results[0], results[1:]
 
 
-def compact_kernel(weights, slot_count, row_count, pivots_ref, *refs):
-    pieces, outs = refs[:-2], refs[-2:]
+def places_kernel(weights, slot_count, row_count, pivots_ref, out_ref):
     panels, width = pivots_ref.shape
-    depth, rows, lanes = pieces[0].shape
-    common = outs[0].shape[0]
+    lanes = panels * slot_count
     shift = row_count.bit_length() - 1
     me = lax.axis_index("rows")
     square = (width, width)
@@ -173,8 +171,27 @@
         for mask, weight in weights:
             block = block + jnp.where((apart & mask) != 0, weight, 0)
         places.append(block * lanes + rank)
-    both = jnp.concatenate([places[0], places[1] + slot_count], 1)
-    halves = jnp.concatenate([places[1], places[1] + slot_count], 1)
+    out_ref[0:1, :] = jnp.concatenate([places[0], places[1] + slot_count], 1)
+    out_ref[1:2, :] = jnp.concatenate([places[1], places[1] + slot_count], 1)
+
+
+def places_of(pivots, weights, slot_count, row_count):
+    return pl.pallas_call(
+        functools.partial(places_kernel, weights, slot_count, row_count),
+        out_shape=jax.ShapeDtypeStruct((2, 2 * pivots.shape[1]), jnp.int32),
+        in_specs=[pl.BlockSpec(memory_space=pltpu.VMEM)],
+        out_specs=pl.BlockSpec(memory_space=pltpu.VMEM),
+        compiler_params=pltpu.CompilerParams(vmem_limit_bytes=16 * MIB),
+        cost_estimate=pl.CostEstimate(flops=MICRO, bytes_accessed=MIB, transcendentals=0),
+        name="places",
+    )(pivots)
+
+
+def compact_kernel(places_ref, *refs):
+    pieces, outs = refs[:-2], refs[-2:]
+    depth, rows, lanes = pieces[0].shape
+    common, width = outs[0].shape
+    both, halves = places_ref[0:1, :], places_ref[1:2, :]
     main = jnp.zeros((common, 2 * width), jnp.float32)
     rest = jnp.zeros((rows - common, 2 * width), jnp.float32)
     for i in range(len(pieces) * depth):
@@ -184,16 +201,16 @@
         rest = rest + dot(x[common:], jnp.where(lane == halves, 1.0, 0.0).astype(jnp.bfloat16))
     outs[0][...] = main[:, :width].astype(jnp.bfloat16)
     outs[1][:common, :] = main[:, width:].astype(jnp.bfloat16)
-    outs[1][common : common + rows - common, :] = rest[:, :width].astype(jnp.bfloat16)
+    outs[1][common:rows, :] = rest[:, :width].astype(jnp.bfloat16)
     outs[1][rows:, :] = rest[:, width:].astype(jnp.bfloat16)
 
 
-def compact(pivots, pieces, weights, slot_count, row_count, part):
-    _, rows, _ = pieces[0].shape
-    width = pivots.shape[1]
+def compact(places, pieces, part):
+    rows = pieces[0].shape[1]
+    width = places.shape[1] // 2
     block_cols = (rows - part) * 2 // 3
     return pl.pallas_call(
-        functools.partial(compact_kernel, weights, slot_count, row_count),
+        compact_kernel,
         out_shape=[
             jax.ShapeDtypeStruct((part + block_cols, width), jnp.bfloat16),
             jax.ShapeDtypeStruct((part + 2 * block_cols, width), jnp.bfloat16),
@@ -203,7 +220,7 @@
         compiler_params=pltpu.CompilerParams(vmem_limit_bytes=16 * MIB),
         cost_estimate=pl.CostEstimate(flops=MICRO, bytes_accessed=MIB, transcendentals=0),
         name="compact",
-    )(pivots, *pieces)
+    )(places, *pieces)
 
 
 def eliminate(block, columns, offset):
@@ -230,8 +247,8 @@
             factor[jv] = jnp.where(sublane > jr, factor[jv], 0.0)
             pivots[first + jv] = jnp.where(sublane == jr, pivot, pivots[first + jv])
             for k in range(j + 1, SUB):
-                entry = jnp.broadcast_to(cols[k][jv][jr : jr + 1, :], (8, LANES))
-                for v in live:
+                entry = jnp.broadcast_to(cols[j][k // 8][k % 8 : k % 8 + 1, :], (8, LANES))
+                for v in range(k // 8, len(diagonal)):
                     cols[k][v] = cols[k][v] - factor[v] * entry
             for rows in tiles.values():
                 entry = jnp.broadcast_to(rows[first + jv][jr : jr + 1, :], (8, LANES))
@@ -386,7 +403,7 @@
     )(work0, *picked0, *picked1)
 
 
-def fourth_kernel(block_cols, work0, before_ref, rows_of, ahead, left, work1):
+def fourth_kernel(apart, block_cols, work0, before_ref, rows_of, ahead, left, work1):
     width = work0.shape[0]
     both = 2 * width
     work1[...] = before_ref[...]
@@ -403,14 +420,23 @@
         ],
         0,
     )
-    left[:, :both] = jnp.concatenate(split(small), 0)
+    ordered = []
+    for panel in range(2):
+        for bits in apart:
+            source = me ^ bits
+            piece = jnp.zeros((2 * block_cols, block_cols), jnp.float32)
+            for block in range(len(apart)):
+                at = panel * width + block * block_cols
+                piece = jnp.where(source == block, small[:, at : at + block_cols], piece)
+            ordered.append(piece)
+    left[:, :both] = jnp.concatenate(split(jnp.concatenate(ordered, 1)), 0)
     left[:, both:] = jnp.concatenate(split(-product_narrow(small, rows_of[...], 1)), 0)
 
 
-def fourth_half(work0, work1, rows_of, ahead, block_cols):
+def fourth_half(work0, work1, rows_of, ahead, apart, block_cols):
     width = work0.shape[0]
     return pl.pallas_call(
-        functools.partial(fourth_kernel, block_cols),
+        functools.partial(fourth_kernel, apart, block_cols),
         out_shape=jax.ShapeDtypeStruct(
             (4 * block_cols, 2 * width + rows_of.shape[0]), jnp.bfloat16
         ),
@@ -423,22 +449,16 @@
     )(work0, work1, rows_of, ahead)
 
 
-def finish_kernel(apart, *refs):
-    count = len(apart)
-    left, vectors_ref = refs[0], refs[1]
-    blocks = refs[2 : 2 + 2 * count]
-    out_ref, right, result, out_sems = refs[2 + 2 * count :]
-    me = lax.axis_index("cols")
+def finish_kernel(left, vectors_ref, *refs):
+    blocks, (out_ref, result, out_sems) = refs[:-3], refs[-3:]
     pairs = vectors_ref.shape[1]
     block_cols = blocks[0].shape[0]
-    both = right.shape[0]
+    both = len(blocks) * block_cols
     outs = []
     for n in range(pairs // CHUNK):
         at = slice(n * CHUNK, (n + 1) * CHUNK)
-        for i, ref in enumerate(blocks):
-            place = i // count * (both // 2) + (me ^ apart[i % count]) * block_cols
-            right[pl.ds(pl.multiple_of(place, block_cols), block_cols), :] = ref[:, at]
-        halves = dot(left[:, both:], vectors_ref[:, at]) + dot(left[:, :both], right[...])
+        right = jnp.concatenate([ref[:, at] for ref in blocks], 0)
+        halves = dot(left[:, both:], vectors_ref[:, at]) + dot(left[:, :both], right)
         value = halves[: 2 * block_cols] + halves[2 * block_cols :]
         result[0, :, at] = value[:block_cols]
         result[1, :, at] = value[block_cols:]
@@ -450,16 +470,14 @@
         copy.wait()
 
 
-def finish(left, vectors, blocks, apart):
+def finish(left, vectors, blocks):
     block_cols, pairs = blocks[0].shape
-    both = left.shape[1] - vectors.shape[0]
-    return pl.pallas_call(
-        functools.partial(finish_kernel, apart),
+    return pl.pallas_call(
+        finish_kernel,
         out_shape=jax.ShapeDtypeStruct((2, block_cols, pairs), jnp.float32),
         in_specs=[pl.BlockSpec(memory_space=pltpu.VMEM)] * (2 + len(blocks)),
         out_specs=pl.BlockSpec(memory_space=pl.ANY),
         scratch_shapes=[
-            pltpu.VMEM((both, CHUNK), jnp.bfloat16),
             pltpu.VMEM((2, block_cols, pairs), jnp.float32),
             pltpu.SemaphoreType.DMA((pairs // CHUNK,)),
         ],
@@ -503,7 +521,8 @@
     for mask in (masks[-2], masks[-1], masks[-2] ^ masks[-1]):
         pieces.append(swap(held, "rows", mask))
         pieces.append(swap(passed, "rows", mask))
-    own0, own1 = compact(pivots, pieces, weights, slot_count, row_count, part)
+    places = places_of(pivots, weights, slot_count, row_count)
+    own0, own1 = compact(places, pieces, part)
 
     far0 = swap(ints[0], "cols", far_mask)
     other0 = swap(own0, "cols", far_mask)
@@ -511,8 +530,7 @@
     picked0 = [own0, other0] + near([own0]) + near([other0])
     beside1 = near([own1])
     beside = near(ints)
-    picked0, last = lax.optimization_barrier((picked0, ints[1]))
-    far1 = swap(last, "cols", far_mask)
+    far1 = swap(ints[1], "cols", far_mask)
     work0 = first_half(picked0, apart, part)
     work0, other1, far0 = lax.optimization_barrier((work0, other1, far0))
     picked1 = [own1, other1] + beside1 + near([other1])
@@ -520,9 +538,9 @@
     work0 = second_half(work0)
     work1, rows_of, ahead = third_half(work0, picked0, picked1, apart, part)
     work1, far1 = lax.optimization_barrier((work1, far1))
-    blocks += [last, far1, beside[1]] + near([far1])
-    left = fourth_half(work0, work1, rows_of, ahead, block_cols)
-    return finish(left, vectors, blocks, apart)
+    blocks += [ints[1], far1, beside[1]] + near([far1])
+    left = fourth_half(work0, work1, rows_of, ahead, apart, block_cols)
+    return finish(left, vectors, blocks)
 
 
 def solution(mesh):

time: 62 us -> 71.3 us (1.15)
  waiting for transfers between devices: 18.6 us -> 27.1 us
    ppermute x19, waiting for transfers between devices: 18.6 us -> 27.1 us  [swap(): return lax.ppermute(x, axis, [(i, i ^ mask) for i in range(size)])]
    pallas_call x3 -> x4, Pallas kernels: 9.56 us -> 10.2 us  [the longest x1 4.82 us: fourth_half(): pl.pallas_call(functools.partial(fourth_kernel, apart, block_cols), out_s...]
  transfers between devices with their start and end apart: 19 -> 19, of which waited for: 9 -> 7; matrix products, arithmetic and copies ran while one was open for 0% -> 0% of each run, Pallas kernels for 26% -> 23%
where the time goes in v2:
time: 71.3 us; the launch traced here: 71.1 us
  waiting for transfers between devices  27.1 us (38%)
  Pallas kernels  25.4 us (36%)
  starting transfers between devices  17.7 us (25%)
    ppermute x19, waiting for transfers between devices, swap(): return lax.ppermute(x, axis, [(i, i ^ mask) for i in range(size)])  27.1 us
    ppermute x19, starting transfers between devices, swap(): return lax.ppermute(x, axis, [(i, i ^ mask) for i in range(size)])  17.7 us
    pallas_call x1, Pallas kernels, fourth_half(): pl.pallas_call(functools.partial(fourth_kernel, apart, block_cols), out_s...  4.82 us
    pallas_call x1, Pallas kernels, third_half(): pl.pallas_call(functools.partial(third_kernel, apart, part), out_shape=[j...  4.59 us
    pallas_call x1, Pallas kernels, finish(): pl.pallas_call(finish_kernel, out_shape=jax.ShapeDtypeStruct((2, block_co...  4.22 us
    pallas_call x1, Pallas kernels, first_half(): pl.pallas_call(functools.partial(first_kernel, apart, part), out_shape=ja...  3.81 us
    pallas_call x1, Pallas kernels, select(): pl.pallas_call(functools.partial(select_kernel, slot_count), out_shape=ou...  3.72 us
    pallas_call x1, Pallas kernels, second_half(): pl.pallas_call(second_kernel, out_shape=jax.ShapeDtypeStruct(work.shape,...  3.04 us
  transfers between devices with their start and end apart: 19, of which 7 were waited for; matrix products, arithmetic and copies ran while one was open for 0% of the time, Pallas kernels for 23%

profile of v2, /device:TPU:0, one launch (start us, length us, event | category | flops | bytes accessed | tf_op | source)
XLA Modules:
  0.0 71.1 jit_solution(16474509291480957832)
XLA Ops:
  0.0 0.7 copy-done
  0.7 3.7 %select.1 = (bf16[352,128]{1,0:T(8,128)(2,1)S(1)}, bf16[64,4096]{1,0:T(8,128)(2,1)S(1)}, bf16[64,4096]{1,0:T(8,128)(2,1)S(1)}) custom-call(s32[2,256]{1,0:T(2,128)S(1)} %copy-done, bf16[1024,4096]{1,0:T(8,128)(2,1)} %vectors_ref.3, bf16[2,64,4096]{2,1,0:T(8,128)(2,1)} %integrals_ref.1), custom_call_target="tpu_custom_call" | custom-call | flops 1073741824 | bytes 3145728 | tf_op jit(solution)/shard_map/select/pallas_call | solution.py:133
  4.4 4.1 %collective-permute-start = (bf16[1,352,128]{2,1,0:T(8,128)(2,1)S(1)}, bf16[1,352,128]{2,1,0:T(8,128)(2,1)S(1)}, u32[]{:S(2)}, u32[]{:S(2)}) collective-permute-start(bf16[1,352,128]{2,1,0:T(8,128)(2,1)S(1)} %bitcast.3), channel_id=1, source_target_pairs={{0,16},{4,20},{8,24},{12,28},{16,0},{20,4},{24,8},{28,12},{1,17},{... | collective-permute-start | bytes 270344 | tf_op jit(solution)/shard_map/ppermute | solution.py:502
  8.5 2.5 %collective-permute-start.5 = (bf16[1,352,128]{2,1,0:T(8,128)(2,1)S(1)}, bf16[1,352,128]{2,1,0:T(8,128)(2,1)S(1)}, u32[]{:S(2)}, u32[]{:S(2)}) collective-permute-start(bf16[1,352,128]{2,1,0:T(8,128)(2,1)S(1)} %bitcast.4), channel_id=1, source_target_pairs={{0,12},{4,8},{8,4},{12,0},{16,28},{20,24},{24,20},{28,16},{1,13},{... | collective-permute-start | bytes 270344 | tf_op jit(solution)/shard_map/ppermute | solution.py:502
  11.0 0.5 collective-permute-start.3
  12.0 0.8 %collective-permute-done.refs_1_ = bf16[1,352,128]{2,1,0:T(8,128)(2,1)S(1)} collective-permute-done((bf16[1,352,128]{2,1,0:T(8,128)(2,1)S(1)}, bf16[1,352,128]{2,1,0:T(8,128)(2,1)S(1)}, u32[]{:S(2)}, u32[]{:S(2)}) %collective-permute-start) | collective-permute-done | bytes 90144 | tf_op jit(solution)/shard_map/ppermute | solution.py:502
  12.8 2.0 %collective-permute-start.6 = (bf16[1,352,128]{2,1,0:T(8,128)(2,1)S(1)}, bf16[1,352,128]{2,1,0:T(8,128)(2,1)S(1)}, u32[]{:S(2)}, u32[]{:S(2)}) collective-permute-start(bf16[1,352,128]{2,1,0:T(8,128)(2,1)S(1)} %collective-permute-done.refs_1_), channel_id=1, source_target_pairs={{0,12},{4,8},{8,4},{12,0},{16,28},{20,24},{24,20},{28,16},{1,13},{... | collective-permute-start | bytes 270344 | tf_op jit(solution)/shard_map/ppermute | solution.py:502
  14.8 0.5 collective-permute-start.4
  15.4 1.4 %collective-permute-start.2 = (bf16[1,352,128]{2,1,0:T(8,128)(2,1)S(1)}, bf16[1,352,128]{2,1,0:T(8,128)(2,1)S(1)}, u32[]{:S(2)}, u32[]{:S(2)}) collective-permute-start(bf16[1,352,128]{2,1,0:T(8,128)(2,1)S(1)} %collective-permute-done.refs_1_), channel_id=1, source_target_pairs={{0,8},{4,12},{8,0},{12,4},{16,24},{20,28},{24,16},{28,20},{1,9},{5... | collective-permute-start | bytes 270344 | tf_op jit(solution)/shard_map/ppermute | solution.py:502
  17.0 1.6 %collective-permute-done.6.refs_7_ = bf16[1,352,128]{2,1,0:T(8,128)(2,1)S(1)} collective-permute-done((bf16[1,352,128]{2,1,0:T(8,128)(2,1)S(1)}, bf16[1,352,128]{2,1,0:T(8,128)(2,1)S(1)}, u32[]{:S(2)}, u32[]{:S(2)}) %collective-permute-start.6) | collective-permute-done | bytes 90144 | tf_op jit(solution)/shard_map/ppermute | solution.py:502
  18.6 1.1 %collective-permute-done.4.refs_5_ = bf16[1,352,128]{2,1,0:T(8,128)(2,1)S(1)} collective-permute-done((bf16[1,352,128]{2,1,0:T(8,128)(2,1)S(1)}, bf16[1,352,128]{2,1,0:T(8,128)(2,1)S(1)}, u32[]{:S(2)}, u32[]{:S(2)}) %collective-permute-start.4) | collective-permute-done | bytes 90144 | tf_op jit(solution)/shard_map/ppermute | solution.py:502
  20.2 1.0 %compact.1 = (bf16[320,256]{1,0:T(8,128)(2,1)S(1)}, bf16[384,256]{1,0:T(8,128)(2,1)S(1)}) custom-call(s32[2,512]{1,0:T(2,128)S(1)} %places.1.places_ref, bf16[1,352,128]{2,1,0:T(8,128)(2,1)S(1)} %bitcast.7, bf16[1,352,128]{2,1,0:T(8,128)(2,1)S(1)} %collective-permute-done.refs_1_, bf16[1,352,128]{2,1,0:T(8,128)(2,1)S(1)} %collective-permute-done.1.refs_2_, ...), custom_call_target="tpu_custom_call" | custom-call | flops 536870912 | bytes 1048576 | tf_op jit(solution)/shard_map/compact/pallas_call | solution.py:212
  21.2 1.6 %collective-permute-start.7 = (bf16[320,256]{1,0:T(8,128)(2,1)S(1)}, bf16[320,256]{1,0:T(8,128)(2,1)S(1)}, u32[]{:S(2)}, u32[]{:S(2)}) collective-permute-start(bf16[320,256]{1,0:T(8,128)(2,1)S(1)} %get-tuple-element.19.refs_0_.refs_1_), channel_id=1, source_target_pairs={{0,2},{1,3},{2,0},{3,1},{4,6},{5,7},{6,4},{7,5},{8,10},{9,11},{10,... | collective-permute-start | bytes 491528 | tf_op jit(solution)/shard_map/ppermute | solution.py:502
  23.3 5.0 %collective-permute-done.7.refs_1_.refs_2_ = bf16[320,256]{1,0:T(8,128)(2,1)S(1)} collective-permute-done((bf16[320,256]{1,0:T(8,128)(2,1)S(1)}, bf16[320,256]{1,0:T(8,128)(2,1)S(1)}, u32[]{:S(2)}, u32[]{:S(2)}) %collective-permute-start.7) | collective-permute-done | bytes 163872 | tf_op jit(solution)/shard_map/ppermute | solution.py:502
  28.8 1.5 %collective-permute-start.14 = (bf16[64,4096]{1,0:T(8,128)(2,1)S(1)}, bf16[64,4096]{1,0:T(8,128)(2,1)S(1)}, u32[]{:S(2)}, u32[]{:S(2)}) collective-permute-start(bf16[64,4096]{1,0:T(8,128)(2,1)S(1)} %get-tuple-element.25.refs_4_), channel_id=1, source_target_pairs={{0,2},{1,3},{2,0},{3,1},{4,6},{5,7},{6,4},{7,5},{8,10},{9,11},{10,... | collective-permute-start | bytes 1572872 | tf_op jit(solution)/shard_map/ppermute | solution.py:502
  30.4 0.9 %collective-permute-start.10 = (bf16[384,256]{1,0:T(8,128)(2,1)S(1)}, bf16[384,256]{1,0:T(8,128)(2,1)S(1)}, u32[]{:S(2)}, u32[]{:S(2)}) collective-permute-start(bf16[384,256]{1,0:T(8,128)(2,1)S(1)} %get-tuple-element.20.refs_5_), channel_id=1, source_target_pairs={{0,2},{1,3},{2,0},{3,1},{4,6},{5,7},{6,4},{7,5},{8,10},{9,11},{10,... | collective-permute-start | bytes 589832 | tf_op jit(solution)/shard_map/ppermute | solution.py:502
  31.2 3.8 %first_half.1.before_ref = f32[256,512]{1,0:T(8,128)S(1)} custom-call(bf16[320,256]{1,0:T(8,128)(2,1)S(1)} %get-tuple-element.19.refs_0_.refs_1_, bf16[320,256]{1,0:T(8,128)(2,1)S(1)} %collective-permute-done.7.refs_1_.refs_2_, bf16[320,256]{1,0:T(8,128)(2,1)S(1)} %collective-permute-done.8.refs_2_.refs_3_, ...), custom_call_target="tpu_custom_call" | custom-call | flops 2147483648 | bytes 1048576 | tf_op jit(solution)/shard_map/first_half/pallas_call | solution.py:334
  35.1 18.0 %collective-permute-done.10.refs_6_ = bf16[384,256]{1,0:T(8,128)(2,1)S(1)} collective-permute-done((bf16[384,256]{1,0:T(8,128)(2,1)S(1)}, bf16[384,256]{1,0:T(8,128)(2,1)S(1)}, u32[]{:S(2)}, u32[]{:S(2)}) %collective-permute-start.10) | collective-permute-done | bytes 196640 | tf_op jit(solution)/shard_map/ppermute | solution.py:502
  53.0 0.5 collective-permute-start.13
  53.5 3.0 %second_half.1.refs_0_.work0 = f32[256,512]{1,0:T(8,128)S(1)} custom-call(f32[256,512]{1,0:T(8,128)S(1)} %first_half.1.before_ref), custom_call_target="tpu_custom_call" | custom-call | flops 2147483648 | bytes 1048576 | tf_op jit(solution)/shard_map/second_half/pallas_call | solution.py:355
  56.7 4.6 %third_half.1 = (f32[256,512]{1,0:T(8,128)S(1)}, bf16[1024,512]{1,0:T(8,128)(2,1)S(1)}, bf16[256,256]{1,0:T(8,128)(2,1)S(1)}) custom-call(f32[256,512]{1,0:T(8,128)S(1)} %second_half.1.refs_0_.work0, bf16[320,256]{1,0:T(8,128)(2,1)S(1)} %get-tuple-element.19.refs_0_.refs_1_, bf16[320,256]{1,0:T(8,128)(2,1)S(1)} %collective-permute-done.7.refs_1_.refs_2_, ...), custom_call_target="tpu_custom_call" | custom-call | flops 2684354560 | bytes 1048576 | tf_op jit(solution)/shard_map/third_half/pallas_call | solution.py:390
  61.3 0.6 collective-permute-start.18
  61.9 4.8 %fourth_half.1.left = bf16[256,1536]{1,0:T(8,128)(2,1)S(1)} custom-call(f32[256,512]{1,0:T(8,128)S(1)} %second_half.1.refs_0_.work0, f32[256,512]{1,0:T(8,128)S(1)} %get-tuple-element.26.before_ref, bf16[1024,512]{1,0:T(8,128)(2,1)S(1)} %get-tuple-element.27.rows_of, bf16[256,256]{1,0:T(8,128)(2,1)S(1)} %get-tuple-element.28.ahead), custom_call_target="tpu_custom_call" | custom-call | flops 2684354560 | bytes 1048576 | tf_op jit(solution)/shard_map/fourth_half/pallas_call | solution.py:438
  66.8 4.2 %finish.1 = f32[2,64,4096]{2,1,0:T(8,128)} custom-call(bf16[256,1536]{1,0:T(8,128)(2,1)S(1)} %fourth_half.1.left, bf16[1024,4096]{1,0:T(8,128)(2,1)S(1)} %bitcast.2, bf16[64,4096]{1,0:T(8,128)(2,1)S(1)} %get-tuple-element.21.refs_0_, bf16[64,4096]{1,0:T(8,128)(2,1)S(1)} %collective-permute-done.11.refs_1_, ...), custom_call_target="tpu_custom_call" | custom-call | flops 3221225472 | bytes 16777216 | tf_op jit(solution)/shard_map/finish/pallas_call | solution.py:475
  (29 shorter events, 2.3 us)
Async XLA Ops:
  0.0 0.7 copy-start
  4.4 8.4 %collective-permute-start = (bf16[1,352,128]{2,1,0:T(8,128)(2,1)S(1)}, bf16[1,352,128]{2,1,0:T(8,128)(2,1)S(1)}, u32[]{:S(2)}, u32[]{:S(2)}) collective-permute-start(bf16[1,352,128]{2,1,0:T(8,128)(2,1)S(1)} %bitcast.3), channel_id=1, source_target_pairs={{0,16},{4,20},{8,24},{12,28},{16,0},{20,4},{24,8},{28,12},{1,17},{... | collective-permute-start | bytes 270344 | tf_op jit(solution)/shard_map/ppermute | solution.py:502
  8.5 6.8 %collective-permute-start.5 = (bf16[1,352,128]{2,1,0:T(8,128)(2,1)S(1)}, bf16[1,352,128]{2,1,0:T(8,128)(2,1)S(1)}, u32[]{:S(2)}, u32[]{:S(2)}) collective-permute-start(bf16[1,352,128]{2,1,0:T(8,128)(2,1)S(1)} %bitcast.4), channel_id=1, source_target_pairs={{0,12},{4,8},{8,4},{12,0},{16,28},{20,24},{24,20},{28,16},{1,13},{... | collective-permute-start | bytes 270344 | tf_op jit(solution)/shard_map/ppermute | solution.py:502
  11.0 5.9 %collective-permute-start.3 = (bf16[1,352,128]{2,1,0:T(8,128)(2,1)S(1)}, bf16[1,352,128]{2,1,0:T(8,128)(2,1)S(1)}, u32[]{:S(2)}, u32[]{:S(2)}) collective-permute-start(bf16[1,352,128]{2,1,0:T(8,128)(2,1)S(1)} %bitcast.5), channel_id=1, source_target_pairs={{0,4},{4,0},{8,12},{12,8},{16,20},{20,16},{24,28},{28,24},{1,5},{5... | collective-permute-start | bytes 270344 | tf_op jit(solution)/shard_map/ppermute | solution.py:502
  11.6 5.5 %collective-permute-start.1 = (bf16[1,352,128]{2,1,0:T(8,128)(2,1)S(1)}, bf16[1,352,128]{2,1,0:T(8,128)(2,1)S(1)}, u32[]{:S(2)}, u32[]{:S(2)}) collective-permute-start(bf16[1,352,128]{2,1,0:T(8,128)(2,1)S(1)} %bitcast.6), channel_id=1, source_target_pairs={{0,8},{4,12},{8,0},{12,4},{16,24},{20,28},{24,16},{28,20},{1,9},{5... | collective-permute-start | bytes 270344 | tf_op jit(solution)/shard_map/ppermute | solution.py:502
  12.8 5.8 %collective-permute-start.6 = (bf16[1,352,128]{2,1,0:T(8,128)(2,1)S(1)}, bf16[1,352,128]{2,1,0:T(8,128)(2,1)S(1)}, u32[]{:S(2)}, u32[]{:S(2)}) collective-permute-start(bf16[1,352,128]{2,1,0:T(8,128)(2,1)S(1)} %collective-permute-done.refs_1_), channel_id=1, source_target_pairs={{0,12},{4,8},{8,4},{12,0},{16,28},{20,24},{24,20},{28,16},{1,13},{... | collective-permute-start | bytes 270344 | tf_op jit(solution)/shard_map/ppermute | solution.py:502
  14.8 4.9 %collective-permute-start.4 = (bf16[1,352,128]{2,1,0:T(8,128)(2,1)S(1)}, bf16[1,352,128]{2,1,0:T(8,128)(2,1)S(1)}, u32[]{:S(2)}, u32[]{:S(2)}) collective-permute-start(bf16[1,352,128]{2,1,0:T(8,128)(2,1)S(1)} %collective-permute-done.refs_1_), channel_id=1, source_target_pairs={{0,4},{4,0},{8,12},{12,8},{16,20},{20,16},{24,28},{28,24},{1,5},{5... | collective-permute-start | bytes 270344 | tf_op jit(solution)/shard_map/ppermute | solution.py:502
  15.4 4.8 %collective-permute-start.2 = (bf16[1,352,128]{2,1,0:T(8,128)(2,1)S(1)}, bf16[1,352,128]{2,1,0:T(8,128)(2,1)S(1)}, u32[]{:S(2)}, u32[]{:S(2)}) collective-permute-start(bf16[1,352,128]{2,1,0:T(8,128)(2,1)S(1)} %collective-permute-done.refs_1_), channel_id=1, source_target_pairs={{0,8},{4,12},{8,0},{12,4},{16,24},{20,28},{24,16},{28,20},{1,9},{5... | collective-permute-start | bytes 270344 | tf_op jit(solution)/shard_map/ppermute | solution.py:502
  21.2 7.1 %collective-permute-start.7 = (bf16[320,256]{1,0:T(8,128)(2,1)S(1)}, bf16[320,256]{1,0:T(8,128)(2,1)S(1)}, u32[]{:S(2)}, u32[]{:S(2)}) collective-permute-start(bf16[320,256]{1,0:T(8,128)(2,1)S(1)} %get-tuple-element.19.refs_0_.refs_1_), channel_id=1, source_target_pairs={{0,2},{1,3},{2,0},{3,1},{4,6},{5,7},{6,4},{7,5},{8,10},{9,11},{10,... | collective-permute-start | bytes 491528 | tf_op jit(solution)/shard_map/ppermute | solution.py:502
  22.8 30.2 %collective-permute-start.11 = (bf16[64,4096]{1,0:T(8,128)(2,1)S(1)}, bf16[64,4096]{1,0:T(8,128)(2,1)S(1)}, u32[]{:S(2)}, u32[]{:S(2)}) collective-permute-start(bf16[64,4096]{1,0:T(8,128)(2,1)S(1)} %get-tuple-element.21.refs_0_), channel_id=1, source_target_pairs={{0,2},{1,3},{2,0},{3,1},{4,6},{5,7},{6,4},{7,5},{8,10},{9,11},{10,... | collective-permute-start | bytes 1572872 | tf_op jit(solution)/shard_map/ppermute | solution.py:502
  23.3 5.6 %collective-permute-start.8 = (bf16[320,256]{1,0:T(8,128)(2,1)S(1)}, bf16[320,256]{1,0:T(8,128)(2,1)S(1)}, u32[]{:S(2)}, u32[]{:S(2)}) collective-permute-start(bf16[320,256]{1,0:T(8,128)(2,1)S(1)} %get-tuple-element.19.refs_0_.refs_1_), channel_id=1, source_target_pairs={{0,1},{1,0},{2,3},{3,2},{4,5},{5,4},{6,7},{7,6},{8,9},{9,8},{10,11... | collective-permute-start | bytes 491528 | tf_op jit(solution)/shard_map/ppermute | solution.py:502
  28.3 2.0 %collective-permute-start.9 = (bf16[320,256]{1,0:T(8,128)(2,1)S(1)}, bf16[320,256]{1,0:T(8,128)(2,1)S(1)}, u32[]{:S(2)}, u32[]{:S(2)}) collective-permute-start(bf16[320,256]{1,0:T(8,128)(2,1)S(1)} %collective-permute-done.7.refs_1_.refs_2_), channel_id=1, source_target_pairs={{0,1},{1,0},{2,3},{3,2},{4,5},{5,4},{6,7},{7,6},{8,9},{9,8},{10,11... | collective-permute-start | bytes 491528 | tf_op jit(solution)/shard_map/ppermute | solution.py:502
  28.3 38.4 %collective-permute-start.15 = (bf16[64,4096]{1,0:T(8,128)(2,1)S(1)}, bf16[64,4096]{1,0:T(8,128)(2,1)S(1)}, u32[]{:S(2)}, u32[]{:S(2)}) collective-permute-start(bf16[64,4096]{1,0:T(8,128)(2,1)S(1)} %get-tuple-element.21.refs_0_), channel_id=1, source_target_pairs={{0,1},{1,0},{2,3},{3,2},{4,5},{5,4},{6,7},{7,6},{8,9},{9,8},{10,11... | collective-permute-start | bytes 1572872 | tf_op jit(solution)/shard_map/ppermute | solution.py:502
  28.8 37.9 %collective-permute-start.17 = (bf16[64,4096]{1,0:T(8,128)(2,1)S(1)}, bf16[64,4096]{1,0:T(8,128)(2,1)S(1)}, u32[]{:S(2)}, u32[]{:S(2)}) collective-permute-start(bf16[64,4096]{1,0:T(8,128)(2,1)S(1)} %get-tuple-element.25.refs_4_), channel_id=1, source_target_pairs={{0,1},{1,0},{2,3},{3,2},{4,5},{5,4},{6,7},{7,6},{8,9},{9,8},{10,11... | collective-permute-start | bytes 1572872 | tf_op jit(solution)/shard_map/ppermute | solution.py:502
  28.8 32.5 %collective-permute-start.14 = (bf16[64,4096]{1,0:T(8,128)(2,1)S(1)}, bf16[64,4096]{1,0:T(8,128)(2,1)S(1)}, u32[]{:S(2)}, u32[]{:S(2)}) collective-permute-start(bf16[64,4096]{1,0:T(8,128)(2,1)S(1)} %get-tuple-element.25.refs_4_), channel_id=1, source_target_pairs={{0,2},{1,3},{2,0},{3,1},{4,6},{5,7},{6,4},{7,5},{8,10},{9,11},{10,... | collective-permute-start | bytes 1572872 | tf_op jit(solution)/shard_map/ppermute | solution.py:502
  30.4 22.6 %collective-permute-start.10 = (bf16[384,256]{1,0:T(8,128)(2,1)S(1)}, bf16[384,256]{1,0:T(8,128)(2,1)S(1)}, u32[]{:S(2)}, u32[]{:S(2)}) collective-permute-start(bf16[384,256]{1,0:T(8,128)(2,1)S(1)} %get-tuple-element.20.refs_5_), channel_id=1, source_target_pairs={{0,2},{1,3},{2,0},{3,1},{4,6},{5,7},{6,4},{7,5},{8,10},{9,11},{10,... | collective-permute-start | bytes 589832 | tf_op jit(solution)/shard_map/ppermute | solution.py:502
  53.0 3.6 %collective-permute-start.12 = (bf16[384,256]{1,0:T(8,128)(2,1)S(1)}, bf16[384,256]{1,0:T(8,128)(2,1)S(1)}, u32[]{:S(2)}, u32[]{:S(2)}) collective-permute-start(bf16[384,256]{1,0:T(8,128)(2,1)S(1)} %get-tuple-element.20.refs_5_), channel_id=1, source_target_pairs={{0,1},{1,0},{2,3},{3,2},{4,5},{5,4},{6,7},{7,6},{8,9},{9,8},{10,11... | collective-permute-start | bytes 589832 | tf_op jit(solution)/shard_map/ppermute | solution.py:502
  53.0 3.7 %collective-permute-start.13 = (bf16[384,256]{1,0:T(8,128)(2,1)S(1)}, bf16[384,256]{1,0:T(8,128)(2,1)S(1)}, u32[]{:S(2)}, u32[]{:S(2)}) collective-permute-start(bf16[384,256]{1,0:T(8,128)(2,1)S(1)} %collective-permute-done.10.refs_6_), channel_id=1, source_target_pairs={{0,1},{1,0},{2,3},{3,2},{4,5},{5,4},{6,7},{7,6},{8,9},{9,8},{10,11... | collective-permute-start | bytes 589832 | tf_op jit(solution)/shard_map/ppermute | solution.py:502
  56.6 10.2 %slice-start = ((s8[8388608]{0:T(1024)(128)(4,1)}), s8[4194304]{0:T(1024)(128)(4,1)S(1)}, s32[]{:S(2)}) async-start(s8[8388608]{0:T(1024)(128)(4,1)} %bitcast.1), calls=%async_computation | async-start | bytes 8388608
  56.6 10.1 %collective-permute-start.16 = (bf16[64,4096]{1,0:T(8,128)(2,1)S(1)}, bf16[64,4096]{1,0:T(8,128)(2,1)S(1)}, u32[]{:S(2)}, u32[]{:S(2)}) collective-permute-start(bf16[64,4096]{1,0:T(8,128)(2,1)S(1)} %collective-permute-done.11.refs_1_), channel_id=1, source_target_pairs={{0,1},{1,0},{2,3},{3,2},{4,5},{5,4},{6,7},{7,6},{8,9},{9,8},{10,11... | collective-permute-start | bytes 1572872 | tf_op jit(solution)/shard_map/ppermute | solution.py:502
  61.3 5.4 %slice-start.1 = ((s8[8388608]{0:T(1024)(128)(4,1)}), s8[4194304]{0:T(1024)(128)(4,1)S(1)}, s32[]{:S(2)}) async-start(s8[8388608]{0:T(1024)(128)(4,1)} %bitcast.1), calls=%async_computation.1 | async-start | bytes 8388608
  61.3 5.4 %collective-permute-start.18 = (bf16[64,4096]{1,0:T(8,128)(2,1)S(1)}, bf16[64,4096]{1,0:T(8,128)(2,1)S(1)}, u32[]{:S(2)}, u32[]{:S(2)}) collective-permute-start(bf16[64,4096]{1,0:T(8,128)(2,1)S(1)} %collective-permute-done.14.refs_5_), channel_id=1, source_target_pairs={{0,1},{1,0},{2,3},{3,2},{4,5},{5,4},{6,7},{7,6},{8,9},{9,8},{10,11... | collective-permute-start | bytes 1572872 | tf_op jit(solution)/shard_map/ppermute | solution.py:502

commit v3 on v2

--- a/solution.py
+++ b/solution.py
@@ -405,32 +405,55 @@
 
 def fourth_kernel(apart, block_cols, work0, before_ref, rows_of, ahead, left, work1):
     width = work0.shape[0]
-    both = 2 * width
-    work1[...] = before_ref[...]
-    run_leaves(work1, width // 2, width)
+    square = (width, width)
     me = lax.axis_index("cols")
     mine = pl.ds(pl.multiple_of(me * block_cols, block_cols), block_cols)
+    work1[...] = before_ref[...]
+    lane = iota(square, 1)
+    source = iota(square, 0)
+    arrive = jnp.zeros(square, jnp.float32)
+    for i, bits in enumerate(apart):
+        shifted = lane + ((me ^ bits) - i) * block_cols
+        here = (lane >= i * block_cols) & (lane < (i + 1) * block_cols)
+        arrive = jnp.where(here & (source == shifted), 1.0, arrive)
+    arrive = arrive.astype(jnp.bfloat16)
+    same = jnp.where(source == lane, 1.0, 0.0).astype(jnp.bfloat16)
+    inverse_high, inverse_low = split(work0[:, width:])
+    through = dot(ahead[...], inverse_high, 0, 0) + dot(ahead[...], inverse_low, 0, 0)
+    through_high, through_low = split(through)
+    early, late = rows_of[:, :width], rows_of[:, width:]
+    on_vectors = dot(
+        jnp.concatenate([same, -through_high, -through_low], 1),
+        jnp.concatenate([late, early, early], 1),
+        1,
+        1,
+    )
+    right_high, right_low = split(
+        jnp.concatenate([-product_narrow(through, arrive), -on_vectors], 1)
+    )
+    right_high = jnp.concatenate([right_high[:, :width], arrive, right_high[:, width:]], 1)
+    right_low = jnp.concatenate(
+        [right_low[:, :width], jnp.zeros_like(arrive), right_low[:, width:]], 1
+    )
+    right = jnp.concatenate([right_high, right_high, right_low], 0)
     inverse0 = work0[mine, width:]
-    inverse1 = work1[mine, width:]
-    through = product_wide(product_narrow(inverse1, ahead[...], 1), work0[:, width:])
-    small = jnp.concatenate(
+    top = jnp.concatenate(
         [
-            jnp.concatenate([inverse0, jnp.zeros_like(inverse0)], 1),
-            jnp.concatenate([-through, inverse1], 1),
+            product_narrow(inverse0, arrive),
+            jnp.zeros((block_cols, width), jnp.float32),
+            -product_narrow(inverse0, early, 1),
         ],
-        0,
-    )
-    ordered = []
-    for panel in range(2):
-        for bits in apart:
-            source = me ^ bits
-            piece = jnp.zeros((2 * block_cols, block_cols), jnp.float32)
-            for block in range(len(apart)):
-                at = panel * width + block * block_cols
-                piece = jnp.where(source == block, small[:, at : at + block_cols], piece)
-            ordered.append(piece)
-    left[:, :both] = jnp.concatenate(split(jnp.concatenate(ordered, 1)), 0)
-    left[:, both:] = jnp.concatenate(split(-product_narrow(small, rows_of[...], 1)), 0)
+        1,
+    )
+    top_high, top_low = split(top)
+    left[:block_cols, :] = top_high
+    left[2 * block_cols : 3 * block_cols, :] = top_low
+
+    run_leaves(work1, width // 2, width)
+    high, low = split(work1[mine, width:])
+    low_high, low_low = split(dot(jnp.concatenate([high, low, high], 1), right))
+    left[block_cols : 2 * block_cols, :] = low_high
+    left[3 * block_cols :, :] = low_low
 
 
 def fourth_half(work0, work1, rows_of, ahead, apart, block_cols):

time: 71.3 us -> 70.4 us (0.987)
  Pallas kernels: 25.4 us -> 24.5 us
    pallas_call x1, Pallas kernels: 4.82 us -> 3.93 us  [fourth_half(): pl.pallas_call(functools.partial(fourth_kernel, apart, block_cols), out_s...]
  transfers between devices with their start and end apart: 19 -> 19, of which waited for: 7 -> 7; matrix products, arithmetic and copies ran while one was open for 0% -> 0% of each run, Pallas kernels for 23% -> 22%
where the time goes in v3:
time: 70.4 us; the launch traced here: 70.3 us
  waiting for transfers between devices  27.1 us (38%)
  Pallas kernels  24.5 us (35%)
  starting transfers between devices  17.7 us (25%)
    ppermute x19, waiting for transfers between devices, swap(): return lax.ppermute(x, axis, [(i, i ^ mask) for i in range(size)])  27.1 us
    ppermute x19, starting transfers between devices, swap(): return lax.ppermute(x, axis, [(i, i ^ mask) for i in range(size)])  17.7 us
    pallas_call x1, Pallas kernels, third_half(): pl.pallas_call(functools.partial(third_kernel, apart, part), out_shape=[j...  4.59 us
    pallas_call x1, Pallas kernels, finish(): pl.pallas_call(finish_kernel, out_shape=jax.ShapeDtypeStruct((2, block_co...  4.22 us
    pallas_call x1, Pallas kernels, fourth_half(): pl.pallas_call(functools.partial(fourth_kernel, apart, block_cols), out_s...  3.93 us
    pallas_call x1, Pallas kernels, first_half(): pl.pallas_call(functools.partial(first_kernel, apart, part), out_shape=ja...  3.81 us
    pallas_call x1, Pallas kernels, select(): pl.pallas_call(functools.partial(select_kernel, slot_count), out_shape=ou...  3.72 us
    pallas_call x1, Pallas kernels, second_half(): pl.pallas_call(second_kernel, out_shape=jax.ShapeDtypeStruct(work.shape,...  3.04 us
  transfers between devices with their start and end apart: 19, of which 7 were waited for; matrix products, arithmetic and copies ran while one was open for 0% of the time, Pallas kernels for 22%

profile of v3, /device:TPU:0, one launch (start us, length us, event | category | flops | bytes accessed | tf_op | source)
XLA Modules:
  0.0 70.3 jit_solution(15040069017746539384)
XLA Ops:
  0.0 0.7 copy-done
  0.7 3.7 %select.1 = (bf16[352,128]{1,0:T(8,128)(2,1)S(1)}, bf16[64,4096]{1,0:T(8,128)(2,1)S(1)}, bf16[64,4096]{1,0:T(8,128)(2,1)S(1)}) custom-call(s32[2,256]{1,0:T(2,128)S(1)} %copy-done, bf16[1024,4096]{1,0:T(8,128)(2,1)} %vectors_ref.3, bf16[2,64,4096]{2,1,0:T(8,128)(2,1)} %integrals_ref.1), custom_call_target="tpu_custom_call" | custom-call | flops 1073741824 | bytes 3145728 | tf_op jit(solution)/shard_map/select/pallas_call | solution.py:133
  4.4 4.1 %collective-permute-start = (bf16[1,352,128]{2,1,0:T(8,128)(2,1)S(1)}, bf16[1,352,128]{2,1,0:T(8,128)(2,1)S(1)}, u32[]{:S(2)}, u32[]{:S(2)}) collective-permute-start(bf16[1,352,128]{2,1,0:T(8,128)(2,1)S(1)} %bitcast.3), channel_id=1, source_target_pairs={{0,16},{4,20},{8,24},{12,28},{16,0},{20,4},{24,8},{28,12},{1,17},{... | collective-permute-start | bytes 270344 | tf_op jit(solution)/shard_map/ppermute | solution.py:525
  8.5 2.5 %collective-permute-start.5 = (bf16[1,352,128]{2,1,0:T(8,128)(2,1)S(1)}, bf16[1,352,128]{2,1,0:T(8,128)(2,1)S(1)}, u32[]{:S(2)}, u32[]{:S(2)}) collective-permute-start(bf16[1,352,128]{2,1,0:T(8,128)(2,1)S(1)} %bitcast.4), channel_id=1, source_target_pairs={{0,12},{4,8},{8,4},{12,0},{16,28},{20,24},{24,20},{28,16},{1,13},{... | collective-permute-start | bytes 270344 | tf_op jit(solution)/shard_map/ppermute | solution.py:525
  11.0 0.5 collective-permute-start.3
  12.0 0.8 %collective-permute-done.refs_1_ = bf16[1,352,128]{2,1,0:T(8,128)(2,1)S(1)} collective-permute-done((bf16[1,352,128]{2,1,0:T(8,128)(2,1)S(1)}, bf16[1,352,128]{2,1,0:T(8,128)(2,1)S(1)}, u32[]{:S(2)}, u32[]{:S(2)}) %collective-permute-start) | collective-permute-done | bytes 90144 | tf_op jit(solution)/shard_map/ppermute | solution.py:525
  12.8 2.0 %collective-permute-start.6 = (bf16[1,352,128]{2,1,0:T(8,128)(2,1)S(1)}, bf16[1,352,128]{2,1,0:T(8,128)(2,1)S(1)}, u32[]{:S(2)}, u32[]{:S(2)}) collective-permute-start(bf16[1,352,128]{2,1,0:T(8,128)(2,1)S(1)} %collective-permute-done.refs_1_), channel_id=1, source_target_pairs={{0,12},{4,8},{8,4},{12,0},{16,28},{20,24},{24,20},{28,16},{1,13},{... | collective-permute-start | bytes 270344 | tf_op jit(solution)/shard_map/ppermute | solution.py:525
  14.8 0.5 collective-permute-start.4
  15.4 1.4 %collective-permute-start.2 = (bf16[1,352,128]{2,1,0:T(8,128)(2,1)S(1)}, bf16[1,352,128]{2,1,0:T(8,128)(2,1)S(1)}, u32[]{:S(2)}, u32[]{:S(2)}) collective-permute-start(bf16[1,352,128]{2,1,0:T(8,128)(2,1)S(1)} %collective-permute-done.refs_1_), channel_id=1, source_target_pairs={{0,8},{4,12},{8,0},{12,4},{16,24},{20,28},{24,16},{28,20},{1,9},{5... | collective-permute-start | bytes 270344 | tf_op jit(solution)/shard_map/ppermute | solution.py:525
  17.0 1.6 %collective-permute-done.6.refs_7_ = bf16[1,352,128]{2,1,0:T(8,128)(2,1)S(1)} collective-permute-done((bf16[1,352,128]{2,1,0:T(8,128)(2,1)S(1)}, bf16[1,352,128]{2,1,0:T(8,128)(2,1)S(1)}, u32[]{:S(2)}, u32[]{:S(2)}) %collective-permute-start.6) | collective-permute-done | bytes 90144 | tf_op jit(solution)/shard_map/ppermute | solution.py:525
  18.6 1.1 %collective-permute-done.4.refs_5_ = bf16[1,352,128]{2,1,0:T(8,128)(2,1)S(1)} collective-permute-done((bf16[1,352,128]{2,1,0:T(8,128)(2,1)S(1)}, bf16[1,352,128]{2,1,0:T(8,128)(2,1)S(1)}, u32[]{:S(2)}, u32[]{:S(2)}) %collective-permute-start.4) | collective-permute-done | bytes 90144 | tf_op jit(solution)/shard_map/ppermute | solution.py:525
  20.2 1.0 %compact.1 = (bf16[320,256]{1,0:T(8,128)(2,1)S(1)}, bf16[384,256]{1,0:T(8,128)(2,1)S(1)}) custom-call(s32[2,512]{1,0:T(2,128)S(1)} %places.1.places_ref, bf16[1,352,128]{2,1,0:T(8,128)(2,1)S(1)} %bitcast.7, bf16[1,352,128]{2,1,0:T(8,128)(2,1)S(1)} %collective-permute-done.refs_1_, bf16[1,352,128]{2,1,0:T(8,128)(2,1)S(1)} %collective-permute-done.1.refs_2_, ...), custom_call_target="tpu_custom_call" | custom-call | flops 536870912 | bytes 1048576 | tf_op jit(solution)/shard_map/compact/pallas_call | solution.py:212
  21.2 1.6 %collective-permute-start.7 = (bf16[320,256]{1,0:T(8,128)(2,1)S(1)}, bf16[320,256]{1,0:T(8,128)(2,1)S(1)}, u32[]{:S(2)}, u32[]{:S(2)}) collective-permute-start(bf16[320,256]{1,0:T(8,128)(2,1)S(1)} %get-tuple-element.19.refs_0_.refs_1_), channel_id=1, source_target_pairs={{0,2},{1,3},{2,0},{3,1},{4,6},{5,7},{6,4},{7,5},{8,10},{9,11},{10,... | collective-permute-start | bytes 491528 | tf_op jit(solution)/shard_map/ppermute | solution.py:525
  23.3 5.0 %collective-permute-done.7.refs_1_.refs_2_ = bf16[320,256]{1,0:T(8,128)(2,1)S(1)} collective-permute-done((bf16[320,256]{1,0:T(8,128)(2,1)S(1)}, bf16[320,256]{1,0:T(8,128)(2,1)S(1)}, u32[]{:S(2)}, u32[]{:S(2)}) %collective-permute-start.7) | collective-permute-done | bytes 163872 | tf_op jit(solution)/shard_map/ppermute | solution.py:525
  28.8 1.5 %collective-permute-start.14 = (bf16[64,4096]{1,0:T(8,128)(2,1)S(1)}, bf16[64,4096]{1,0:T(8,128)(2,1)S(1)}, u32[]{:S(2)}, u32[]{:S(2)}) collective-permute-start(bf16[64,4096]{1,0:T(8,128)(2,1)S(1)} %get-tuple-element.25.refs_4_), channel_id=1, source_target_pairs={{0,2},{1,3},{2,0},{3,1},{4,6},{5,7},{6,4},{7,5},{8,10},{9,11},{10,... | collective-permute-start | bytes 1572872 | tf_op jit(solution)/shard_map/ppermute | solution.py:525
  30.4 0.9 %collective-permute-start.10 = (bf16[384,256]{1,0:T(8,128)(2,1)S(1)}, bf16[384,256]{1,0:T(8,128)(2,1)S(1)}, u32[]{:S(2)}, u32[]{:S(2)}) collective-permute-start(bf16[384,256]{1,0:T(8,128)(2,1)S(1)} %get-tuple-element.20.refs_5_), channel_id=1, source_target_pairs={{0,2},{1,3},{2,0},{3,1},{4,6},{5,7},{6,4},{7,5},{8,10},{9,11},{10,... | collective-permute-start | bytes 589832 | tf_op jit(solution)/shard_map/ppermute | solution.py:525
  31.2 3.8 %first_half.1.before_ref = f32[256,512]{1,0:T(8,128)S(1)} custom-call(bf16[320,256]{1,0:T(8,128)(2,1)S(1)} %get-tuple-element.19.refs_0_.refs_1_, bf16[320,256]{1,0:T(8,128)(2,1)S(1)} %collective-permute-done.7.refs_1_.refs_2_, bf16[320,256]{1,0:T(8,128)(2,1)S(1)} %collective-permute-done.8.refs_2_.refs_3_, ...), custom_call_target="tpu_custom_call" | custom-call | flops 2147483648 | bytes 1048576 | tf_op jit(solution)/shard_map/first_half/pallas_call | solution.py:334
  35.1 18.0 %collective-permute-done.10.refs_6_ = bf16[384,256]{1,0:T(8,128)(2,1)S(1)} collective-permute-done((bf16[384,256]{1,0:T(8,128)(2,1)S(1)}, bf16[384,256]{1,0:T(8,128)(2,1)S(1)}, u32[]{:S(2)}, u32[]{:S(2)}) %collective-permute-start.10) | collective-permute-done | bytes 196640 | tf_op jit(solution)/shard_map/ppermute | solution.py:525
  53.0 0.5 collective-permute-start.13
  53.5 3.0 %second_half.1.refs_0_.work0 = f32[256,512]{1,0:T(8,128)S(1)} custom-call(f32[256,512]{1,0:T(8,128)S(1)} %first_half.1.before_ref), custom_call_target="tpu_custom_call" | custom-call | flops 2147483648 | bytes 1048576 | tf_op jit(solution)/shard_map/second_half/pallas_call | solution.py:355
  56.7 4.6 %third_half.1 = (f32[256,512]{1,0:T(8,128)S(1)}, bf16[1024,512]{1,0:T(8,128)(2,1)S(1)}, bf16[256,256]{1,0:T(8,128)(2,1)S(1)}) custom-call(f32[256,512]{1,0:T(8,128)S(1)} %second_half.1.refs_0_.work0, bf16[320,256]{1,0:T(8,128)(2,1)S(1)} %get-tuple-element.19.refs_0_.refs_1_, bf16[320,256]{1,0:T(8,128)(2,1)S(1)} %collective-permute-done.7.refs_1_.refs_2_, ...), custom_call_target="tpu_custom_call" | custom-call | flops 2684354560 | bytes 1048576 | tf_op jit(solution)/shard_map/third_half/pallas_call | solution.py:390
  61.3 0.6 collective-permute-start.18
  61.9 3.9 %fourth_half.1.left = bf16[256,1536]{1,0:T(8,128)(2,1)S(1)} custom-call(f32[256,512]{1,0:T(8,128)S(1)} %second_half.1.refs_0_.work0, f32[256,512]{1,0:T(8,128)S(1)} %get-tuple-element.26.before_ref, bf16[1024,512]{1,0:T(8,128)(2,1)S(1)} %get-tuple-element.27.rows_of, bf16[256,256]{1,0:T(8,128)(2,1)S(1)} %get-tuple-element.28.ahead), custom_call_target="tpu_custom_call" | custom-call | flops 2684354560 | bytes 1048576 | tf_op jit(solution)/shard_map/fourth_half/pallas_call | solution.py:461
  65.9 4.2 %finish.1 = f32[2,64,4096]{2,1,0:T(8,128)} custom-call(bf16[256,1536]{1,0:T(8,128)(2,1)S(1)} %fourth_half.1.left, bf16[1024,4096]{1,0:T(8,128)(2,1)S(1)} %bitcast.2, bf16[64,4096]{1,0:T(8,128)(2,1)S(1)} %get-tuple-element.21.refs_0_, bf16[64,4096]{1,0:T(8,128)(2,1)S(1)} %collective-permute-done.11.refs_1_, ...), custom_call_target="tpu_custom_call" | custom-call | flops 3221225472 | bytes 16777216 | tf_op jit(solution)/shard_map/finish/pallas_call | solution.py:498
  (29 shorter events, 2.3 us)
Async XLA Ops:
  0.0 0.7 copy-start
  4.4 8.4 %collective-permute-start = (bf16[1,352,128]{2,1,0:T(8,128)(2,1)S(1)}, bf16[1,352,128]{2,1,0:T(8,128)(2,1)S(1)}, u32[]{:S(2)}, u32[]{:S(2)}) collective-permute-start(bf16[1,352,128]{2,1,0:T(8,128)(2,1)S(1)} %bitcast.3), channel_id=1, source_target_pairs={{0,16},{4,20},{8,24},{12,28},{16,0},{20,4},{24,8},{28,12},{1,17},{... | collective-permute-start | bytes 270344 | tf_op jit(solution)/shard_map/ppermute | solution.py:525
  8.5 6.8 %collective-permute-start.5 = (bf16[1,352,128]{2,1,0:T(8,128)(2,1)S(1)}, bf16[1,352,128]{2,1,0:T(8,128)(2,1)S(1)}, u32[]{:S(2)}, u32[]{:S(2)}) collective-permute-start(bf16[1,352,128]{2,1,0:T(8,128)(2,1)S(1)} %bitcast.4), channel_id=1, source_target_pairs={{0,12},{4,8},{8,4},{12,0},{16,28},{20,24},{24,20},{28,16},{1,13},{... | collective-permute-start | bytes 270344 | tf_op jit(solution)/shard_map/ppermute | solution.py:525
  11.0 5.9 %collective-permute-start.3 = (bf16[1,352,128]{2,1,0:T(8,128)(2,1)S(1)}, bf16[1,352,128]{2,1,0:T(8,128)(2,1)S(1)}, u32[]{:S(2)}, u32[]{:S(2)}) collective-permute-start(bf16[1,352,128]{2,1,0:T(8,128)(2,1)S(1)} %bitcast.5), channel_id=1, source_target_pairs={{0,4},{4,0},{8,12},{12,8},{16,20},{20,16},{24,28},{28,24},{1,5},{5... | collective-permute-start | bytes 270344 | tf_op jit(solution)/shard_map/ppermute | solution.py:525
  11.6 5.5 %collective-permute-start.1 = (bf16[1,352,128]{2,1,0:T(8,128)(2,1)S(1)}, bf16[1,352,128]{2,1,0:T(8,128)(2,1)S(1)}, u32[]{:S(2)}, u32[]{:S(2)}) collective-permute-start(bf16[1,352,128]{2,1,0:T(8,128)(2,1)S(1)} %bitcast.6), channel_id=1, source_target_pairs={{0,8},{4,12},{8,0},{12,4},{16,24},{20,28},{24,16},{28,20},{1,9},{5... | collective-permute-start | bytes 270344 | tf_op jit(solution)/shard_map/ppermute | solution.py:525
  12.8 5.8 %collective-permute-start.6 = (bf16[1,352,128]{2,1,0:T(8,128)(2,1)S(1)}, bf16[1,352,128]{2,1,0:T(8,128)(2,1)S(1)}, u32[]{:S(2)}, u32[]{:S(2)}) collective-permute-start(bf16[1,352,128]{2,1,0:T(8,128)(2,1)S(1)} %collective-permute-done.refs_1_), channel_id=1, source_target_pairs={{0,12},{4,8},{8,4},{12,0},{16,28},{20,24},{24,20},{28,16},{1,13},{... | collective-permute-start | bytes 270344 | tf_op jit(solution)/shard_map/ppermute | solution.py:525
  14.8 4.9 %collective-permute-start.4 = (bf16[1,352,128]{2,1,0:T(8,128)(2,1)S(1)}, bf16[1,352,128]{2,1,0:T(8,128)(2,1)S(1)}, u32[]{:S(2)}, u32[]{:S(2)}) collective-permute-start(bf16[1,352,128]{2,1,0:T(8,128)(2,1)S(1)} %collective-permute-done.refs_1_), channel_id=1, source_target_pairs={{0,4},{4,0},{8,12},{12,8},{16,20},{20,16},{24,28},{28,24},{1,5},{5... | collective-permute-start | bytes 270344 | tf_op jit(solution)/shard_map/ppermute | solution.py:525
  15.4 4.8 %collective-permute-start.2 = (bf16[1,352,128]{2,1,0:T(8,128)(2,1)S(1)}, bf16[1,352,128]{2,1,0:T(8,128)(2,1)S(1)}, u32[]{:S(2)}, u32[]{:S(2)}) collective-permute-start(bf16[1,352,128]{2,1,0:T(8,128)(2,1)S(1)} %collective-permute-done.refs_1_), channel_id=1, source_target_pairs={{0,8},{4,12},{8,0},{12,4},{16,24},{20,28},{24,16},{28,20},{1,9},{5... | collective-permute-start | bytes 270344 | tf_op jit(solution)/shard_map/ppermute | solution.py:525
  21.2 7.1 %collective-permute-start.7 = (bf16[320,256]{1,0:T(8,128)(2,1)S(1)}, bf16[320,256]{1,0:T(8,128)(2,1)S(1)}, u32[]{:S(2)}, u32[]{:S(2)}) collective-permute-start(bf16[320,256]{1,0:T(8,128)(2,1)S(1)} %get-tuple-element.19.refs_0_.refs_1_), channel_id=1, source_target_pairs={{0,2},{1,3},{2,0},{3,1},{4,6},{5,7},{6,4},{7,5},{8,10},{9,11},{10,... | collective-permute-start | bytes 491528 | tf_op jit(solution)/shard_map/ppermute | solution.py:525
  22.8 30.2 %collective-permute-start.11 = (bf16[64,4096]{1,0:T(8,128)(2,1)S(1)}, bf16[64,4096]{1,0:T(8,128)(2,1)S(1)}, u32[]{:S(2)}, u32[]{:S(2)}) collective-permute-start(bf16[64,4096]{1,0:T(8,128)(2,1)S(1)} %get-tuple-element.21.refs_0_), channel_id=1, source_target_pairs={{0,2},{1,3},{2,0},{3,1},{4,6},{5,7},{6,4},{7,5},{8,10},{9,11},{10,... | collective-permute-start | bytes 1572872 | tf_op jit(solution)/shard_map/ppermute | solution.py:525
  23.3 5.6 %collective-permute-start.8 = (bf16[320,256]{1,0:T(8,128)(2,1)S(1)}, bf16[320,256]{1,0:T(8,128)(2,1)S(1)}, u32[]{:S(2)}, u32[]{:S(2)}) collective-permute-start(bf16[320,256]{1,0:T(8,128)(2,1)S(1)} %get-tuple-element.19.refs_0_.refs_1_), channel_id=1, source_target_pairs={{0,1},{1,0},{2,3},{3,2},{4,5},{5,4},{6,7},{7,6},{8,9},{9,8},{10,11... | collective-permute-start | bytes 491528 | tf_op jit(solution)/shard_map/ppermute | solution.py:525
  28.3 2.0 %collective-permute-start.9 = (bf16[320,256]{1,0:T(8,128)(2,1)S(1)}, bf16[320,256]{1,0:T(8,128)(2,1)S(1)}, u32[]{:S(2)}, u32[]{:S(2)}) collective-permute-start(bf16[320,256]{1,0:T(8,128)(2,1)S(1)} %collective-permute-done.7.refs_1_.refs_2_), channel_id=1, source_target_pairs={{0,1},{1,0},{2,3},{3,2},{4,5},{5,4},{6,7},{7,6},{8,9},{9,8},{10,11... | collective-permute-start | bytes 491528 | tf_op jit(solution)/shard_map/ppermute | solution.py:525
  28.3 37.5 %collective-permute-start.15 = (bf16[64,4096]{1,0:T(8,128)(2,1)S(1)}, bf16[64,4096]{1,0:T(8,128)(2,1)S(1)}, u32[]{:S(2)}, u32[]{:S(2)}) collective-permute-start(bf16[64,4096]{1,0:T(8,128)(2,1)S(1)} %get-tuple-element.21.refs_0_), channel_id=1, source_target_pairs={{0,1},{1,0},{2,3},{3,2},{4,5},{5,4},{6,7},{7,6},{8,9},{9,8},{10,11... | collective-permute-start | bytes 1572872 | tf_op jit(solution)/shard_map/ppermute | solution.py:525
  28.8 37.0 %collective-permute-start.17 = (bf16[64,4096]{1,0:T(8,128)(2,1)S(1)}, bf16[64,4096]{1,0:T(8,128)(2,1)S(1)}, u32[]{:S(2)}, u32[]{:S(2)}) collective-permute-start(bf16[64,4096]{1,0:T(8,128)(2,1)S(1)} %get-tuple-element.25.refs_4_), channel_id=1, source_target_pairs={{0,1},{1,0},{2,3},{3,2},{4,5},{5,4},{6,7},{7,6},{8,9},{9,8},{10,11... | collective-permute-start | bytes 1572872 | tf_op jit(solution)/shard_map/ppermute | solution.py:525
  28.8 32.5 %collective-permute-start.14 = (bf16[64,4096]{1,0:T(8,128)(2,1)S(1)}, bf16[64,4096]{1,0:T(8,128)(2,1)S(1)}, u32[]{:S(2)}, u32[]{:S(2)}) collective-permute-start(bf16[64,4096]{1,0:T(8,128)(2,1)S(1)} %get-tuple-element.25.refs_4_), channel_id=1, source_target_pairs={{0,2},{1,3},{2,0},{3,1},{4,6},{5,7},{6,4},{7,5},{8,10},{9,11},{10,... | collective-permute-start | bytes 1572872 | tf_op jit(solution)/shard_map/ppermute | solution.py:525
  30.4 22.6 %collective-permute-start.10 = (bf16[384,256]{1,0:T(8,128)(2,1)S(1)}, bf16[384,256]{1,0:T(8,128)(2,1)S(1)}, u32[]{:S(2)}, u32[]{:S(2)}) collective-permute-start(bf16[384,256]{1,0:T(8,128)(2,1)S(1)} %get-tuple-element.20.refs_5_), channel_id=1, source_target_pairs={{0,2},{1,3},{2,0},{3,1},{4,6},{5,7},{6,4},{7,5},{8,10},{9,11},{10,... | collective-permute-start | bytes 589832 | tf_op jit(solution)/shard_map/ppermute | solution.py:525
  53.0 3.6 %collective-permute-start.12 = (bf16[384,256]{1,0:T(8,128)(2,1)S(1)}, bf16[384,256]{1,0:T(8,128)(2,1)S(1)}, u32[]{:S(2)}, u32[]{:S(2)}) collective-permute-start(bf16[384,256]{1,0:T(8,128)(2,1)S(1)} %get-tuple-element.20.refs_5_), channel_id=1, source_target_pairs={{0,1},{1,0},{2,3},{3,2},{4,5},{5,4},{6,7},{7,6},{8,9},{9,8},{10,11... | collective-permute-start | bytes 589832 | tf_op jit(solution)/shard_map/ppermute | solution.py:525
  53.0 3.7 %collective-permute-start.13 = (bf16[384,256]{1,0:T(8,128)(2,1)S(1)}, bf16[384,256]{1,0:T(8,128)(2,1)S(1)}, u32[]{:S(2)}, u32[]{:S(2)}) collective-permute-start(bf16[384,256]{1,0:T(8,128)(2,1)S(1)} %collective-permute-done.10.refs_6_), channel_id=1, source_target_pairs={{0,1},{1,0},{2,3},{3,2},{4,5},{5,4},{6,7},{7,6},{8,9},{9,8},{10,11... | collective-permute-start | bytes 589832 | tf_op jit(solution)/shard_map/ppermute | solution.py:525
  56.6 9.3 %slice-start = ((s8[8388608]{0:T(1024)(128)(4,1)}), s8[4194304]{0:T(1024)(128)(4,1)S(1)}, s32[]{:S(2)}) async-start(s8[8388608]{0:T(1024)(128)(4,1)} %bitcast.1), calls=%async_computation | async-start | bytes 8388608
  56.6 9.2 %collective-permute-start.16 = (bf16[64,4096]{1,0:T(8,128)(2,1)S(1)}, bf16[64,4096]{1,0:T(8,128)(2,1)S(1)}, u32[]{:S(2)}, u32[]{:S(2)}) collective-permute-start(bf16[64,4096]{1,0:T(8,128)(2,1)S(1)} %collective-permute-done.11.refs_1_), channel_id=1, source_target_pairs={{0,1},{1,0},{2,3},{3,2},{4,5},{5,4},{6,7},{7,6},{8,9},{9,8},{10,11... | collective-permute-start | bytes 1572872 | tf_op jit(solution)/shard_map/ppermute | solution.py:525
  61.3 4.6 %slice-start.1 = ((s8[8388608]{0:T(1024)(128)(4,1)}), s8[4194304]{0:T(1024)(128)(4,1)S(1)}, s32[]{:S(2)}) async-start(s8[8388608]{0:T(1024)(128)(4,1)} %bitcast.1), calls=%async_computation.1 | async-start | bytes 8388608
  61.3 4.5 %collective-permute-start.18 = (bf16[64,4096]{1,0:T(8,128)(2,1)S(1)}, bf16[64,4096]{1,0:T(8,128)(2,1)S(1)}, u32[]{:S(2)}, u32[]{:S(2)}) collective-permute-start(bf16[64,4096]{1,0:T(8,128)(2,1)S(1)} %collective-permute-done.14.refs_5_), channel_id=1, source_target_pairs={{0,1},{1,0},{2,3},{3,2},{4,5},{5,4},{6,7},{7,6},{8,9},{9,8},{10,11... | collective-permute-start | bytes 1572872 | tf_op jit(solution)/shard_map/ppermute | solution.py:525

commit v4 on v3

--- a/solution.py
+++ b/solution.py
@@ -477,14 +477,26 @@
     pairs = vectors_ref.shape[1]
     block_cols = blocks[0].shape[0]
     both = len(blocks) * block_cols
+    second = jnp.concatenate(
+        [
+            left[block_cols : 2 * block_cols, both // 2 : both],
+            left[3 * block_cols :, both // 2 : both],
+        ],
+        0,
+    )
     outs = []
     for n in range(pairs // CHUNK):
         at = slice(n * CHUNK, (n + 1) * CHUNK)
-        right = jnp.concatenate([ref[:, at] for ref in blocks], 0)
-        halves = dot(left[:, both:], vectors_ref[:, at]) + dot(left[:, :both], right)
+        right0, right1 = (
+            jnp.concatenate([ref[:, at] for ref in some], 0)
+            for some in (blocks[: len(blocks) // 2], blocks[len(blocks) // 2 :])
+        )
+        halves = dot(left[:, both:], vectors_ref[:, at]) + dot(left[:, : both // 2], right0)
         value = halves[: 2 * block_cols] + halves[2 * block_cols :]
+        halves = dot(second, right1)
+        last = value[block_cols:] + (halves[:block_cols] + halves[block_cols:])
         result[0, :, at] = value[:block_cols]
-        result[1, :, at] = value[block_cols:]
+        result[1, :, at] = last
         outs.append(
             pltpu.make_async_copy(result.at[:, :, at], out_ref.at[:, :, at], out_sems.at[n])
         )
@@ -555,7 +567,7 @@
     beside = near(ints)
     far1 = swap(ints[1], "cols", far_mask)
     work0 = first_half(picked0, apart, part)
-    work0, other1, far0 = lax.optimization_barrier((work0, other1, far0))
+    work0, other1 = lax.optimization_barrier((work0, other1))
     picked1 = [own1, other1] + beside1 + near([other1])
     blocks = [ints[0], far0, beside[0]] + near([far0])
     work0 = second_half(work0)

time: 70.4 us -> 73.5 us (1.044)
  waiting for transfers between devices: 27.1 us -> 30 us
    ppermute x19, waiting for transfers between devices: 27.1 us -> 30 us  [swap(): return lax.ppermute(x, axis, [(i, i ^ mask) for i in range(size)])]
  transfers between devices with their start and end apart: 19 -> 19, of which waited for: 7 -> 7; matrix products, arithmetic and copies ran while one was open for 0% -> 0% of each run, Pallas kernels for 22% -> 21%
where the time goes in v4:
time: 73.5 us; the launch traced here: 73.3 us
  waiting for transfers between devices  30 us (41%)
  Pallas kernels  24.2 us (33%)
  starting transfers between devices  18.1 us (25%)
    ppermute x19, waiting for transfers between devices, swap(): return lax.ppermute(x, axis, [(i, i ^ mask) for i in range(size)])  30 us
    ppermute x19, starting transfers between devices, swap(): return lax.ppermute(x, axis, [(i, i ^ mask) for i in range(size)])  18.1 us
    pallas_call x1, Pallas kernels, third_half(): pl.pallas_call(functools.partial(third_kernel, apart, part), out_shape=[j...  4.59 us
    pallas_call x1, Pallas kernels, finish(): pl.pallas_call(finish_kernel, out_shape=jax.ShapeDtypeStruct((2, block_co...  3.94 us
    pallas_call x1, Pallas kernels, fourth_half(): pl.pallas_call(functools.partial(fourth_kernel, apart, block_cols), out_s...  3.93 us
    pallas_call x1, Pallas kernels, first_half(): pl.pallas_call(functools.partial(first_kernel, apart, part), out_shape=ja...  3.81 us
    pallas_call x1, Pallas kernels, select(): pl.pallas_call(functools.partial(select_kernel, slot_count), out_shape=ou...  3.72 us
    pallas_call x1, Pallas kernels, second_half(): pl.pallas_call(second_kernel, out_shape=jax.ShapeDtypeStruct(work.shape,...  3.05 us
  transfers between devices with their start and end apart: 19, of which 7 were waited for; matrix products, arithmetic and copies ran while one was open for 0% of the time, Pallas kernels for 21%

profile of v4, /device:TPU:0, one launch (start us, length us, event | category | flops | bytes accessed | tf_op | source)
XLA Modules:
  0.0 73.3 jit_solution(17216451915178437288)
XLA Ops:
  0.0 0.7 copy-done
  0.7 3.7 %select.1 = (bf16[352,128]{1,0:T(8,128)(2,1)S(1)}, bf16[64,4096]{1,0:T(8,128)(2,1)S(1)}, bf16[64,4096]{1,0:T(8,128)(2,1)S(1)}) custom-call(s32[2,256]{1,0:T(2,128)S(1)} %copy-done, bf16[1024,4096]{1,0:T(8,128)(2,1)} %vectors_ref.3, bf16[2,64,4096]{2,1,0:T(8,128)(2,1)} %integrals_ref.1), custom_call_target="tpu_custom_call" | custom-call | flops 1073741824 | bytes 3145728 | tf_op jit(solution)/shard_map/select/pallas_call | solution.py:133
  4.4 4.1 %collective-permute-start = (bf16[1,352,128]{2,1,0:T(8,128)(2,1)S(1)}, bf16[1,352,128]{2,1,0:T(8,128)(2,1)S(1)}, u32[]{:S(2)}, u32[]{:S(2)}) collective-permute-start(bf16[1,352,128]{2,1,0:T(8,128)(2,1)S(1)} %bitcast.3), channel_id=1, source_target_pairs={{0,16},{4,20},{8,24},{12,28},{16,0},{20,4},{24,8},{28,12},{1,17},{... | collective-permute-start | bytes 270344 | tf_op jit(solution)/shard_map/ppermute | solution.py:537
  8.5 2.5 %collective-permute-start.5 = (bf16[1,352,128]{2,1,0:T(8,128)(2,1)S(1)}, bf16[1,352,128]{2,1,0:T(8,128)(2,1)S(1)}, u32[]{:S(2)}, u32[]{:S(2)}) collective-permute-start(bf16[1,352,128]{2,1,0:T(8,128)(2,1)S(1)} %bitcast.4), channel_id=1, source_target_pairs={{0,12},{4,8},{8,4},{12,0},{16,28},{20,24},{24,20},{28,16},{1,13},{... | collective-permute-start | bytes 270344 | tf_op jit(solution)/shard_map/ppermute | solution.py:537
  11.0 0.5 collective-permute-start.3
  12.0 0.8 %collective-permute-done.refs_1_ = bf16[1,352,128]{2,1,0:T(8,128)(2,1)S(1)} collective-permute-done((bf16[1,352,128]{2,1,0:T(8,128)(2,1)S(1)}, bf16[1,352,128]{2,1,0:T(8,128)(2,1)S(1)}, u32[]{:S(2)}, u32[]{:S(2)}) %collective-permute-start) | collective-permute-done | bytes 90144 | tf_op jit(solution)/shard_map/ppermute | solution.py:537
  12.8 2.0 %collective-permute-start.6 = (bf16[1,352,128]{2,1,0:T(8,128)(2,1)S(1)}, bf16[1,352,128]{2,1,0:T(8,128)(2,1)S(1)}, u32[]{:S(2)}, u32[]{:S(2)}) collective-permute-start(bf16[1,352,128]{2,1,0:T(8,128)(2,1)S(1)} %collective-permute-done.refs_1_), channel_id=1, source_target_pairs={{0,12},{4,8},{8,4},{12,0},{16,28},{20,24},{24,20},{28,16},{1,13},{... | collective-permute-start | bytes 270344 | tf_op jit(solution)/shard_map/ppermute | solution.py:537
  14.8 0.5 collective-permute-start.4
  15.4 1.4 %collective-permute-start.2 = (bf16[1,352,128]{2,1,0:T(8,128)(2,1)S(1)}, bf16[1,352,128]{2,1,0:T(8,128)(2,1)S(1)}, u32[]{:S(2)}, u32[]{:S(2)}) collective-permute-start(bf16[1,352,128]{2,1,0:T(8,128)(2,1)S(1)} %collective-permute-done.refs_1_), channel_id=1, source_target_pairs={{0,8},{4,12},{8,0},{12,4},{16,24},{20,28},{24,16},{28,20},{1,9},{5... | collective-permute-start | bytes 270344 | tf_op jit(solution)/shard_map/ppermute | solution.py:537
  17.0 1.6 %collective-permute-done.6.refs_7_ = bf16[1,352,128]{2,1,0:T(8,128)(2,1)S(1)} collective-permute-done((bf16[1,352,128]{2,1,0:T(8,128)(2,1)S(1)}, bf16[1,352,128]{2,1,0:T(8,128)(2,1)S(1)}, u32[]{:S(2)}, u32[]{:S(2)}) %collective-permute-start.6) | collective-permute-done | bytes 90144 | tf_op jit(solution)/shard_map/ppermute | solution.py:537
  18.6 1.1 %collective-permute-done.4.refs_5_ = bf16[1,352,128]{2,1,0:T(8,128)(2,1)S(1)} collective-permute-done((bf16[1,352,128]{2,1,0:T(8,128)(2,1)S(1)}, bf16[1,352,128]{2,1,0:T(8,128)(2,1)S(1)}, u32[]{:S(2)}, u32[]{:S(2)}) %collective-permute-start.4) | collective-permute-done | bytes 90144 | tf_op jit(solution)/shard_map/ppermute | solution.py:537
  20.2 1.0 %compact.1 = (bf16[320,256]{1,0:T(8,128)(2,1)S(1)}, bf16[384,256]{1,0:T(8,128)(2,1)S(1)}) custom-call(s32[2,512]{1,0:T(2,128)S(1)} %places.1.places_ref, bf16[1,352,128]{2,1,0:T(8,128)(2,1)S(1)} %bitcast.7, bf16[1,352,128]{2,1,0:T(8,128)(2,1)S(1)} %collective-permute-done.refs_1_, bf16[1,352,128]{2,1,0:T(8,128)(2,1)S(1)} %collective-permute-done.1.refs_2_, ...), custom_call_target="tpu_custom_call" | custom-call | flops 536870912 | bytes 1048576 | tf_op jit(solution)/shard_map/compact/pallas_call | solution.py:212
  21.2 1.6 %collective-permute-start.7 = (bf16[320,256]{1,0:T(8,128)(2,1)S(1)}, bf16[320,256]{1,0:T(8,128)(2,1)S(1)}, u32[]{:S(2)}, u32[]{:S(2)}) collective-permute-start(bf16[320,256]{1,0:T(8,128)(2,1)S(1)} %get-tuple-element.18.refs_0_.refs_1_), channel_id=1, source_target_pairs={{0,2},{1,3},{2,0},{3,1},{4,6},{5,7},{6,4},{7,5},{8,10},{9,11},{10,... | collective-permute-start | bytes 491528 | tf_op jit(solution)/shard_map/ppermute | solution.py:537
  22.8 3.8 %collective-permute-done.7.refs_1_.refs_2_ = bf16[320,256]{1,0:T(8,128)(2,1)S(1)} collective-permute-done((bf16[320,256]{1,0:T(8,128)(2,1)S(1)}, bf16[320,256]{1,0:T(8,128)(2,1)S(1)}, u32[]{:S(2)}, u32[]{:S(2)}) %collective-permute-start.7) | collective-permute-done | bytes 163872 | tf_op jit(solution)/shard_map/ppermute | solution.py:537
  26.6 1.5 %collective-permute-start.14 = (bf16[64,4096]{1,0:T(8,128)(2,1)S(1)}, bf16[64,4096]{1,0:T(8,128)(2,1)S(1)}, u32[]{:S(2)}, u32[]{:S(2)}) collective-permute-start(bf16[64,4096]{1,0:T(8,128)(2,1)S(1)} %get-tuple-element.27.refs_0_), channel_id=1, source_target_pairs={{0,2},{1,3},{2,0},{3,1},{4,6},{5,7},{6,4},{7,5},{8,10},{9,11},{10,... | collective-permute-start | bytes 1572872 | tf_op jit(solution)/shard_map/ppermute | solution.py:537
  28.3 0.5 collective-permute-start.13
  28.8 1.6 %collective-permute-start.10 = (bf16[384,256]{1,0:T(8,128)(2,1)S(1)}, bf16[384,256]{1,0:T(8,128)(2,1)S(1)}, u32[]{:S(2)}, u32[]{:S(2)}) collective-permute-start(bf16[384,256]{1,0:T(8,128)(2,1)S(1)} %get-tuple-element.19.refs_5_), channel_id=1, source_target_pairs={{0,2},{1,3},{2,0},{3,1},{4,6},{5,7},{6,4},{7,5},{8,10},{9,11},{10,... | collective-permute-start | bytes 589832 | tf_op jit(solution)/shard_map/ppermute | solution.py:537
  30.4 3.8 %first_half.1.before_ref = f32[256,512]{1,0:T(8,128)S(1)} custom-call(bf16[320,256]{1,0:T(8,128)(2,1)S(1)} %get-tuple-element.18.refs_0_.refs_1_, bf16[320,256]{1,0:T(8,128)(2,1)S(1)} %collective-permute-done.7.refs_1_.refs_2_, bf16[320,256]{1,0:T(8,128)(2,1)S(1)} %collective-permute-done.8.refs_2_.refs_3_, ...), custom_call_target="tpu_custom_call" | custom-call | flops 2147483648 | bytes 1048576 | tf_op jit(solution)/shard_map/first_half/pallas_call | solution.py:334
  34.3 22.1 %collective-permute-done.10.refs_6_ = bf16[384,256]{1,0:T(8,128)(2,1)S(1)} collective-permute-done((bf16[384,256]{1,0:T(8,128)(2,1)S(1)}, bf16[384,256]{1,0:T(8,128)(2,1)S(1)}, u32[]{:S(2)}, u32[]{:S(2)}) %collective-permute-start.10) | collective-permute-done | bytes 196640 | tf_op jit(solution)/shard_map/ppermute | solution.py:537
  56.4 3.0 %second_half.1.refs_0_.work0 = f32[256,512]{1,0:T(8,128)S(1)} custom-call(f32[256,512]{1,0:T(8,128)S(1)} %first_half.1.before_ref), custom_call_target="tpu_custom_call" | custom-call | flops 2147483648 | bytes 1048576 | tf_op jit(solution)/shard_map/second_half/pallas_call | solution.py:355
  59.4 0.6 collective-permute-start.15
  60.1 4.6 %third_half.1 = (f32[256,512]{1,0:T(8,128)S(1)}, bf16[1024,512]{1,0:T(8,128)(2,1)S(1)}, bf16[256,256]{1,0:T(8,128)(2,1)S(1)}) custom-call(f32[256,512]{1,0:T(8,128)S(1)} %second_half.1.refs_0_.work0, bf16[320,256]{1,0:T(8,128)(2,1)S(1)} %get-tuple-element.18.refs_0_.refs_1_, bf16[320,256]{1,0:T(8,128)(2,1)S(1)} %collective-permute-done.7.refs_1_.refs_2_, ...), custom_call_target="tpu_custom_call" | custom-call | flops 2684354560 | bytes 1048576 | tf_op jit(solution)/shard_map/third_half/pallas_call | solution.py:390
  65.2 3.9 %fourth_half.1.left = bf16[256,1536]{1,0:T(8,128)(2,1)S(1)} custom-call(f32[256,512]{1,0:T(8,128)S(1)} %second_half.1.refs_0_.work0, f32[256,512]{1,0:T(8,128)S(1)} %get-tuple-element.24.before_ref, bf16[1024,512]{1,0:T(8,128)(2,1)S(1)} %get-tuple-element.25.rows_of, bf16[256,256]{1,0:T(8,128)(2,1)S(1)} %get-tuple-element.26.ahead), custom_call_target="tpu_custom_call" | custom-call | flops 2684354560 | bytes 1048576 | tf_op jit(solution)/shard_map/fourth_half/pallas_call | solution.py:461
  69.2 3.9 %finish.1 = f32[2,64,4096]{2,1,0:T(8,128)} custom-call(bf16[256,1536]{1,0:T(8,128)(2,1)S(1)} %fourth_half.1.left, bf16[1024,4096]{1,0:T(8,128)(2,1)S(1)} %bitcast.2, bf16[64,4096]{1,0:T(8,128)(2,1)S(1)} %get-tuple-element.27.refs_0_, bf16[64,4096]{1,0:T(8,128)(2,1)S(1)} %collective-permute-done.14.refs_1_, ...), custom_call_target="tpu_custom_call" | custom-call | flops 3221225472 | bytes 16777216 | tf_op jit(solution)/shard_map/finish/pallas_call | solution.py:510
  (29 shorter events, 2.0 us)
Async XLA Ops:
  0.0 0.7 copy-start
  4.4 8.4 %collective-permute-start = (bf16[1,352,128]{2,1,0:T(8,128)(2,1)S(1)}, bf16[1,352,128]{2,1,0:T(8,128)(2,1)S(1)}, u32[]{:S(2)}, u32[]{:S(2)}) collective-permute-start(bf16[1,352,128]{2,1,0:T(8,128)(2,1)S(1)} %bitcast.3), channel_id=1, source_target_pairs={{0,16},{4,20},{8,24},{12,28},{16,0},{20,4},{24,8},{28,12},{1,17},{... | collective-permute-start | bytes 270344 | tf_op jit(solution)/shard_map/ppermute | solution.py:537
  8.5 6.8 %collective-permute-start.5 = (bf16[1,352,128]{2,1,0:T(8,128)(2,1)S(1)}, bf16[1,352,128]{2,1,0:T(8,128)(2,1)S(1)}, u32[]{:S(2)}, u32[]{:S(2)}) collective-permute-start(bf16[1,352,128]{2,1,0:T(8,128)(2,1)S(1)} %bitcast.4), channel_id=1, source_target_pairs={{0,12},{4,8},{8,4},{12,0},{16,28},{20,24},{24,20},{28,16},{1,13},{... | collective-permute-start | bytes 270344 | tf_op jit(solution)/shard_map/ppermute | solution.py:537
  11.0 5.9 %collective-permute-start.3 = (bf16[1,352,128]{2,1,0:T(8,128)(2,1)S(1)}, bf16[1,352,128]{2,1,0:T(8,128)(2,1)S(1)}, u32[]{:S(2)}, u32[]{:S(2)}) collective-permute-start(bf16[1,352,128]{2,1,0:T(8,128)(2,1)S(1)} %bitcast.5), channel_id=1, source_target_pairs={{0,4},{4,0},{8,12},{12,8},{16,20},{20,16},{24,28},{28,24},{1,5},{5... | collective-permute-start | bytes 270344 | tf_op jit(solution)/shard_map/ppermute | solution.py:537
  11.6 5.5 %collective-permute-start.1 = (bf16[1,352,128]{2,1,0:T(8,128)(2,1)S(1)}, bf16[1,352,128]{2,1,0:T(8,128)(2,1)S(1)}, u32[]{:S(2)}, u32[]{:S(2)}) collective-permute-start(bf16[1,352,128]{2,1,0:T(8,128)(2,1)S(1)} %bitcast.6), channel_id=1, source_target_pairs={{0,8},{4,12},{8,0},{12,4},{16,24},{20,28},{24,16},{28,20},{1,9},{5... | collective-permute-start | bytes 270344 | tf_op jit(solution)/shard_map/ppermute | solution.py:537
  12.8 5.8 %collective-permute-start.6 = (bf16[1,352,128]{2,1,0:T(8,128)(2,1)S(1)}, bf16[1,352,128]{2,1,0:T(8,128)(2,1)S(1)}, u32[]{:S(2)}, u32[]{:S(2)}) collective-permute-start(bf16[1,352,128]{2,1,0:T(8,128)(2,1)S(1)} %collective-permute-done.refs_1_), channel_id=1, source_target_pairs={{0,12},{4,8},{8,4},{12,0},{16,28},{20,24},{24,20},{28,16},{1,13},{... | collective-permute-start | bytes 270344 | tf_op jit(solution)/shard_map/ppermute | solution.py:537
  14.8 4.9 %collective-permute-start.4 = (bf16[1,352,128]{2,1,0:T(8,128)(2,1)S(1)}, bf16[1,352,128]{2,1,0:T(8,128)(2,1)S(1)}, u32[]{:S(2)}, u32[]{:S(2)}) collective-permute-start(bf16[1,352,128]{2,1,0:T(8,128)(2,1)S(1)} %collective-permute-done.refs_1_), channel_id=1, source_target_pairs={{0,4},{4,0},{8,12},{12,8},{16,20},{20,16},{24,28},{28,24},{1,5},{5... | collective-permute-start | bytes 270344 | tf_op jit(solution)/shard_map/ppermute | solution.py:537
  15.4 4.8 %collective-permute-start.2 = (bf16[1,352,128]{2,1,0:T(8,128)(2,1)S(1)}, bf16[1,352,128]{2,1,0:T(8,128)(2,1)S(1)}, u32[]{:S(2)}, u32[]{:S(2)}) collective-permute-start(bf16[1,352,128]{2,1,0:T(8,128)(2,1)S(1)} %collective-permute-done.refs_1_), channel_id=1, source_target_pairs={{0,8},{4,12},{8,0},{12,4},{16,24},{20,28},{24,16},{28,20},{1,9},{5... | collective-permute-start | bytes 270344 | tf_op jit(solution)/shard_map/ppermute | solution.py:537
  21.2 5.4 %collective-permute-start.7 = (bf16[320,256]{1,0:T(8,128)(2,1)S(1)}, bf16[320,256]{1,0:T(8,128)(2,1)S(1)}, u32[]{:S(2)}, u32[]{:S(2)}) collective-permute-start(bf16[320,256]{1,0:T(8,128)(2,1)S(1)} %get-tuple-element.18.refs_0_.refs_1_), channel_id=1, source_target_pairs={{0,2},{1,3},{2,0},{3,1},{4,6},{5,7},{6,4},{7,5},{8,10},{9,11},{10,... | collective-permute-start | bytes 491528 | tf_op jit(solution)/shard_map/ppermute | solution.py:537
  22.8 6.1 %collective-permute-start.8 = (bf16[320,256]{1,0:T(8,128)(2,1)S(1)}, bf16[320,256]{1,0:T(8,128)(2,1)S(1)}, u32[]{:S(2)}, u32[]{:S(2)}) collective-permute-start(bf16[320,256]{1,0:T(8,128)(2,1)S(1)} %get-tuple-element.18.refs_0_.refs_1_), channel_id=1, source_target_pairs={{0,1},{1,0},{2,3},{3,2},{4,5},{5,4},{6,7},{7,6},{8,9},{9,8},{10,11... | collective-permute-start | bytes 491528 | tf_op jit(solution)/shard_map/ppermute | solution.py:537
  26.6 2.3 %collective-permute-start.9 = (bf16[320,256]{1,0:T(8,128)(2,1)S(1)}, bf16[320,256]{1,0:T(8,128)(2,1)S(1)}, u32[]{:S(2)}, u32[]{:S(2)}) collective-permute-start(bf16[320,256]{1,0:T(8,128)(2,1)S(1)} %collective-permute-done.7.refs_1_.refs_2_), channel_id=1, source_target_pairs={{0,1},{1,0},{2,3},{3,2},{4,5},{5,4},{6,7},{7,6},{8,9},{9,8},{10,11... | collective-permute-start | bytes 491528 | tf_op jit(solution)/shard_map/ppermute | solution.py:537
  26.6 33.4 %collective-permute-start.14 = (bf16[64,4096]{1,0:T(8,128)(2,1)S(1)}, bf16[64,4096]{1,0:T(8,128)(2,1)S(1)}, u32[]{:S(2)}, u32[]{:S(2)}) collective-permute-start(bf16[64,4096]{1,0:T(8,128)(2,1)S(1)} %get-tuple-element.27.refs_0_), channel_id=1, source_target_pairs={{0,2},{1,3},{2,0},{3,1},{4,6},{5,7},{6,4},{7,5},{8,10},{9,11},{10,... | collective-permute-start | bytes 1572872 | tf_op jit(solution)/shard_map/ppermute | solution.py:537
  28.1 41.1 %collective-permute-start.17 = (bf16[64,4096]{1,0:T(8,128)(2,1)S(1)}, bf16[64,4096]{1,0:T(8,128)(2,1)S(1)}, u32[]{:S(2)}, u32[]{:S(2)}) collective-permute-start(bf16[64,4096]{1,0:T(8,128)(2,1)S(1)} %get-tuple-element.23.refs_4_), channel_id=1, source_target_pairs={{0,1},{1,0},{2,3},{3,2},{4,5},{5,4},{6,7},{7,6},{8,9},{9,8},{10,11... | collective-permute-start | bytes 1572872 | tf_op jit(solution)/shard_map/ppermute | solution.py:537
  28.3 36.4 %collective-permute-start.13 = (bf16[64,4096]{1,0:T(8,128)(2,1)S(1)}, bf16[64,4096]{1,0:T(8,128)(2,1)S(1)}, u32[]{:S(2)}, u32[]{:S(2)}) collective-permute-start(bf16[64,4096]{1,0:T(8,128)(2,1)S(1)} %get-tuple-element.23.refs_4_), channel_id=1, source_target_pairs={{0,2},{1,3},{2,0},{3,1},{4,6},{5,7},{6,4},{7,5},{8,10},{9,11},{10,... | collective-permute-start | bytes 1572872 | tf_op jit(solution)/shard_map/ppermute | solution.py:537
  28.8 30.6 %collective-permute-start.11 = (bf16[384,256]{1,0:T(8,128)(2,1)S(1)}, bf16[384,256]{1,0:T(8,128)(2,1)S(1)}, u32[]{:S(2)}, u32[]{:S(2)}) collective-permute-start(bf16[384,256]{1,0:T(8,128)(2,1)S(1)} %get-tuple-element.19.refs_5_), channel_id=1, source_target_pairs={{0,1},{1,0},{2,3},{3,2},{4,5},{5,4},{6,7},{7,6},{8,9},{9,8},{10,11... | collective-permute-start | bytes 589832 | tf_op jit(solution)/shard_map/ppermute | solution.py:537
  28.8 27.5 %collective-permute-start.10 = (bf16[384,256]{1,0:T(8,128)(2,1)S(1)}, bf16[384,256]{1,0:T(8,128)(2,1)S(1)}, u32[]{:S(2)}, u32[]{:S(2)}) collective-permute-start(bf16[384,256]{1,0:T(8,128)(2,1)S(1)} %get-tuple-element.19.refs_5_), channel_id=1, source_target_pairs={{0,2},{1,3},{2,0},{3,1},{4,6},{5,7},{6,4},{7,5},{8,10},{9,11},{10,... | collective-permute-start | bytes 589832 | tf_op jit(solution)/shard_map/ppermute | solution.py:537
  56.4 3.7 %collective-permute-start.12 = (bf16[384,256]{1,0:T(8,128)(2,1)S(1)}, bf16[384,256]{1,0:T(8,128)(2,1)S(1)}, u32[]{:S(2)}, u32[]{:S(2)}) collective-permute-start(bf16[384,256]{1,0:T(8,128)(2,1)S(1)} %collective-permute-done.10.refs_6_), channel_id=1, source_target_pairs={{0,1},{1,0},{2,3},{3,2},{4,5},{5,4},{6,7},{7,6},{8,9},{9,8},{10,11... | collective-permute-start | bytes 589832 | tf_op jit(solution)/shard_map/ppermute | solution.py:537
  59.4 9.8 %slice-start = ((s8[8388608]{0:T(1024)(128)(4,1)}), s8[4194304]{0:T(1024)(128)(4,1)S(1)}, s32[]{:S(2)}) async-start(s8[8388608]{0:T(1024)(128)(4,1)} %bitcast.1), calls=%async_computation | async-start | bytes 8388608
  59.4 9.7 %collective-permute-start.15 = (bf16[64,4096]{1,0:T(8,128)(2,1)S(1)}, bf16[64,4096]{1,0:T(8,128)(2,1)S(1)}, u32[]{:S(2)}, u32[]{:S(2)}) collective-permute-start(bf16[64,4096]{1,0:T(8,128)(2,1)S(1)} %get-tuple-element.27.refs_0_), channel_id=1, source_target_pairs={{0,1},{1,0},{2,3},{3,2},{4,5},{5,4},{6,7},{7,6},{8,9},{9,8},{10,11... | collective-permute-start | bytes 1572872 | tf_op jit(solution)/shard_map/ppermute | solution.py:537
  60.0 9.2 %collective-permute-start.16 = (bf16[64,4096]{1,0:T(8,128)(2,1)S(1)}, bf16[64,4096]{1,0:T(8,128)(2,1)S(1)}, u32[]{:S(2)}, u32[]{:S(2)}) collective-permute-start(bf16[64,4096]{1,0:T(8,128)(2,1)S(1)} %collective-permute-done.14.refs_1_), channel_id=1, source_target_pairs={{0,1},{1,0},{2,3},{3,2},{4,5},{5,4},{6,7},{7,6},{8,9},{9,8},{10,11... | collective-permute-start | bytes 1572872 | tf_op jit(solution)/shard_map/ppermute | solution.py:537
  64.7 4.5 %slice-start.1 = ((s8[8388608]{0:T(1024)(128)(4,1)}), s8[4194304]{0:T(1024)(128)(4,1)S(1)}, s32[]{:S(2)}) async-start(s8[8388608]{0:T(1024)(128)(4,1)} %bitcast.1), calls=%async_computation.1 | async-start | bytes 8388608
  64.7 4.5 %collective-permute-start.18 = (bf16[64,4096]{1,0:T(8,128)(2,1)S(1)}, bf16[64,4096]{1,0:T(8,128)(2,1)S(1)}, u32[]{:S(2)}, u32[]{:S(2)}) collective-permute-start(bf16[64,4096]{1,0:T(8,128)(2,1)S(1)} %collective-permute-done.13.refs_5_), channel_id=1, source_target_pairs={{0,1},{1,0},{2,3},{3,2},{4,5},{5,4},{6,7},{7,6},{8,9},{9,8},{10,11... | collective-permute-start | bytes 1572872 | tf_op jit(solution)/shard_map/ppermute | solution.py:537
